TPU v7x, 32 devices: a whole 2x2x4 slice. The times are simulated.
32 devices in a mesh: dp: 2 (over x), sp: 16 (over z, y, core).
Axes of the slice: x: 2, y: 2, z: 4, core: 2. Of those that a mesh axis runs over, the one named last changes fastest.
Arguments:
- atom_act: bfloat16 [64, 1024, 128], P('dp', 'sp'), parts along dimension 0
- cond: bfloat16 [1024, 128], P('sp')
- pair: bfloat16 [32, 32, 128, 16], P('sp')
- atom_mask: int32 [1024], P('sp')
- w_cond: bfloat16 [3, 128, 768], replicated
- b_cond: float32 [3, 512], replicated
- w_qkvg: bfloat16 [3, 128, 512], replicated
- b_query: float32 [3, 128], replicated
- w_pair: bfloat16 [16, 12], replicated
- w_out: bfloat16 [3, 128, 128], replicated
- w_up: bfloat16 [3, 128, 512], replicated
- w_down: bfloat16 [3, 256, 128], replicated
Outputs:
- output: bfloat16 [64, 1024, 128], P('dp', 'sp'), parts along dimension 0
There are 2 independent parts. A program takes and returns all parts, laid end to end along the dimension named above; an argument that names none is the same for every part.
All inputs are finite; a program needn't handle non-finite values.
Results may differ from a plain program's by a relative error of at most 0.0131585.
Values are sent between devices in bfloat16 or wider.
A program may use at most 1 GiB of HBM per device.

v0:
```python
import functools
import math

import jax
import jax.numpy as jnp
from jax import lax
from jax.experimental import pallas as pl
from jax.experimental.pallas import tpu as pltpu
from jax.sharding import PartitionSpec as P

QBLOCK = 32
KEY_WINDOW = 128
EDGE = 48
LN_EPS = 1e-5
GROUP = 4
LOG2E = math.log2(math.e)
NT = (((1,), (1,)), ((), ()))
MESH = pl.DeviceIdType.MESH


def mm(lhs, rhs):
    return jnp.dot(lhs, rhs, preferred_element_type=jnp.float32)


def mm_nt(lhs, rhs):
    return lax.dot_general(lhs, rhs, NT, preferred_element_type=jnp.float32)


def sigmoid(vals):
    return 0.5 * jnp.tanh(0.5 * vals) + 0.5


def norm(vals, axis):
    mean = jnp.mean(vals, axis=axis, keepdims=True)
    cent = vals - mean
    var = jnp.mean(cent * cent, axis=axis, keepdims=True)
    return cent * lax.rsqrt(var + LN_EPS)


def body(n_dev, act_hbm, cond_ref, pair_hbm, mask_ref, wcond_hbm, bcond_ref, wqkvg_hbm, bquery_ref, wpair_ref,
         wout_hbm, wup_hbm, wdown_hbm, out_ref,
         act, pair, wcond, wqkvg, wout, wup, wdown,
         pairf, res, h_cm, h_ext, tab, bias, wv_t, wg_t, wo_t, wu_t, wd_t,
         k_scr, q_scr, v_scr, o_scr, mask_buf,
         in_sem, send_sem, recv_sem, msend_sem, mrecv_sem):
    n_layers, width = bquery_ref.shape
    n_heads = width // QBLOCK
    head_dim = width // n_heads
    n_groups = act.shape[0] // GROUP
    seq = act.shape[1]
    ext = seq + 2 * EDGE
    f32, bf16 = jnp.float32, jnp.bfloat16

    me = lax.axis_index('sp')
    nxt = lax.rem(me + 1, n_dev)
    prv = lax.rem(me + n_dev - 1, n_dev)

    loads = [pltpu.make_async_copy(src, dst, in_sem.at[pos]) for pos, (src, dst) in enumerate(
        [(wcond_hbm, wcond), (act_hbm, act), (pair_hbm, pair), (wqkvg_hbm, wqkvg),
         (wout_hbm, wout), (wup_hbm, wup), (wdown_hbm, wdown)])]
    for load in loads:
        load.start()

    barrier = pltpu.get_barrier_semaphore()
    for peer in (prv, nxt):
        pl.semaphore_signal(barrier, inc=1, device_id={'sp': peer}, device_id_type=MESH)

    mask_buf[1] = jnp.zeros_like(mask_buf[1])
    mask_buf[1, 0:1, 0:seq] = mask_ref[...]

    cond_norm = norm(cond_ref[...].astype(f32), -1).astype(bf16)
    loads[0].wait()

    def tables(layer):
        proj = mm(cond_norm, wcond[layer])
        gates = bcond_ref[layer]
        pieces = []
        for idx, bias_idx in enumerate((0, None, 1, 2, None, 3)):
            piece = proj[:, idx * width:(idx + 1) * width]
            if bias_idx is not None:
                piece = sigmoid(piece + gates[:, bias_idx * width:(bias_idx + 1) * width])
            pieces.append(piece)
        for idx, piece in enumerate(pieces):
            for blk in range(2):
                rows = piece[blk * QBLOCK:(blk + 1) * QBLOCK]
                tab[layer, idx, :, blk * 128:(blk + 1) * 128] = jnp.concatenate([rows] * GROUP, axis=0).T

    tables(0)
    pl.semaphore_wait(barrier, 2)

    def mask_copy(direction):
        return pltpu.make_async_remote_copy(
            src_ref=mask_buf.at[1], dst_ref=mask_buf.at[2 - 2 * direction],
            send_sem=msend_sem.at[direction], recv_sem=mrecv_sem.at[direction],
            device_id={'sp': nxt if direction else prv}, device_id_type=MESH)

    def halo_copy(layer, grp, direction):
        samples = pl.ds(grp * GROUP, GROUP)
        src = pl.ds(seq if direction else EDGE, EDGE)
        dst = pl.ds(0 if direction else seq + EDGE, EDGE)
        return pltpu.make_async_remote_copy(
            src_ref=h_ext.at[layer, samples, src, :], dst_ref=h_ext.at[layer, samples, dst, :],
            send_sem=send_sem.at[layer, grp, direction], recv_sem=recv_sem.at[layer, grp, direction],
            device_id={'sp': nxt if direction else prv}, device_id_type=MESH)

    for direction in range(2):
        mask_copy(direction).start()

    def emit_h(layer, grp, resid):
        h_t = (norm(resid, 0) * tab[layer, 0] + tab[layer, 1]).astype(bf16)
        h_cm[grp] = h_t
        for blk in range(2):
            h_nat = h_t[:, blk * 128:(blk + 1) * 128].T
            for smp in range(GROUP):
                h_ext[layer, grp * GROUP + smp, EDGE + blk * QBLOCK:EDGE + (blk + 1) * QBLOCK, :] = (
                    h_nat[smp * QBLOCK:(smp + 1) * QBLOCK])
        for direction in range(2):
            halo_copy(layer, grp, direction).start()

    loads[1].wait()

    @pl.loop(0, n_groups)
    def _(grp):
        rows = act[pl.ds(grp * GROUP, GROUP)].astype(f32)
        cols = [rows[:, blk * QBLOCK:(blk + 1) * QBLOCK].reshape(128, width).T for blk in range(2)]
        resid = jnp.concatenate(cols, axis=1)
        res[grp] = resid
        emit_h(0, grp, resid)

    @pl.loop(1, n_layers)
    def _(layer):
        tables(layer)

    loads[3].wait()
    loads[4].wait()
    loads[5].wait()
    loads[6].wait()

    @pl.loop(0, n_layers)
    def _(layer):
        wv_t[layer] = wqkvg[layer, :, 2 * width:3 * width].T
        wg_t[layer] = wqkvg[layer, :, 3 * width:].T
        wo_t[layer] = wout[layer].T
        for idx in range(4):
            wu_t[layer, idx * width:(idx + 1) * width, :] = wup[layer, :, idx * width:(idx + 1) * width].T
        for idx in range(2):
            wd_t[layer, :, idx * width:(idx + 1) * width] = wdown[layer, idx * width:(idx + 1) * width, :].T

    loads[2].wait()
    pairf[...] = pair[...].astype(f32)
    for direction in range(2):
        mask_copy(direction).wait_recv()
    mask_prev = jnp.where(me > 0, mask_buf[0, 0:1, :], 0)
    mask_next = jnp.where(me < n_dev - 1, mask_buf[2, 0:1, :], 0)
    mask_own = mask_buf[1, 0:1, :]
    ext_mask = jnp.concatenate(
        [mask_prev[:, seq - EDGE:seq], mask_own[:, :seq], mask_next[:, :EDGE], jnp.zeros((1, 256 - ext), jnp.int32)], axis=1)
    ext_bias = (ext_mask.astype(f32) - 1.0) * 1e9
    wpair = wpair_ref[...].astype(f32)
    c_pair = wpair.shape[0]
    for blk in range(2):
        planes = [pairf[pl.ds(blk * QBLOCK * c_pair + chan, QBLOCK, stride=c_pair), :] for chan in range(c_pair)]
        mean = functools.reduce(jnp.add, planes) * (1.0 / c_pair)
        planes = [plane - mean for plane in planes]
        var = functools.reduce(jnp.add, [plane * plane for plane in planes]) * (1.0 / c_pair)
        rstd = lax.rsqrt(var + LN_EPS)
        planes = [(plane * rstd).astype(bf16).astype(f32) for plane in planes]
        mask_row = ext_bias[:, blk * QBLOCK:blk * QBLOCK + KEY_WINDOW]
        for layer in range(n_layers):
            heads = []
            for head in range(n_heads):
                col = layer * n_heads + head
                val = functools.reduce(jnp.add, [
                    planes[chan] * wpair[chan:chan + 1, col:col + 1] for chan in range(c_pair)])
                heads.append(val.astype(bf16).astype(f32))
            table = (jnp.concatenate(heads, axis=0) + mask_row) * LOG2E
            table = table.T
            for smp in range(GROUP):
                bias[layer, smp, blk] = table if smp == 0 else pltpu.roll(table, smp * QBLOCK, 1)

    lane = lax.broadcasted_iota(jnp.int32, (1, width), 1)
    head_of_lane = lane // head_dim
    scale = head_dim ** -0.5 * LOG2E

    def step(layer, grp, last):
        for direction in range(2):
            halo_copy(layer, grp, direction).wait_recv()
        w_qk = wqkvg[layer, :, :2 * width]
        b_q = bquery_ref[pl.ds(layer, 1), :]
        w_v = wv_t[layer]
        for smp in range(GROUP):
            h_nat = h_ext[layer, grp * GROUP + smp]
            q_k = mm(h_nat, w_qk)
            k_scr[smp] = q_k[:, width:].astype(bf16)
            q_val = (q_k[EDGE:EDGE + seq, :width] + b_q).astype(bf16)
            for blk in range(2):
                rows = q_val[blk * QBLOCK:(blk + 1) * QBLOCK]
                for slot in range(n_heads):
                    head = (slot - smp) % n_heads
                    q_scr[smp, blk * 128 + slot * QBLOCK:blk * 128 + (slot + 1) * QBLOCK, :] = jnp.where(
                        head_of_lane == head, rows, jnp.zeros_like(rows))
            v_scr[smp] = mm_nt(w_v, h_nat).astype(bf16)
        for smp in range(GROUP):
            logits = mm_nt(k_scr[smp], q_scr[smp])
            probs = []
            for blk in range(2):
                x = logits[blk * QBLOCK:blk * QBLOCK + KEY_WINDOW, blk * 128:(blk + 1) * 128] * scale + bias[layer, smp, blk]
                e = jnp.exp2(x - jnp.max(x, axis=0, keepdims=True))
                p = (e * (1.0 / jnp.sum(e, axis=0, keepdims=True))).astype(bf16)
                zero = jnp.zeros((QBLOCK, 128), bf16)
                probs.append(jnp.concatenate([zero, p] if blk else [p, zero], axis=0))
            o_t = mm(v_scr[smp], jnp.concatenate(probs, axis=1))
            for head in range(n_heads):
                slot = (head + smp) % n_heads
                rows = slice(head * head_dim, (head + 1) * head_dim)
                for blk in range(2):
                    cols = slice(blk * 128, (blk + 1) * 128)
                    part = o_t[rows, cols]
                    if smp == 0:
                        o_scr[rows, cols] = part
                    else:
                        o_scr[rows, cols] = jnp.where(lane // QBLOCK == slot, part, o_scr[rows, cols])
        gate = sigmoid(mm(wg_t[layer], h_cm[grp]))
        heads = []
        for head in range(n_heads):
            rows = slice(head * head_dim, (head + 1) * head_dim)
            parts = []
            for blk in range(2):
                part = o_scr[rows, blk * 128:(blk + 1) * 128]
                parts.append(pltpu.roll(part, (128 - head * QBLOCK) % 128, 1) if head else part)
            heads.append(jnp.concatenate(parts, axis=1))
        o_val = (gate * jnp.concatenate(heads, axis=0)).astype(bf16)
        resid = res[grp] + tab[layer, 2] * mm(wo_t[layer], o_val)
        h_t = (norm(resid, 0) * tab[layer, 3] + tab[layer, 4]).astype(bf16)
        up = mm(wu_t[layer], h_t)
        left, right = up[:2 * width], up[2 * width:]
        half = 0.5 * left
        hidden = ((half * jnp.tanh(half) + half) * right).astype(bf16)
        resid = resid + tab[layer, 5] * mm(wd_t[layer], hidden)
        if last:
            for blk in range(2):
                nat = resid[:, blk * 128:(blk + 1) * 128].T.astype(bf16)
                for smp in range(GROUP):
                    out_ref[grp * GROUP + smp, blk * QBLOCK:(blk + 1) * QBLOCK, :] = nat[smp * QBLOCK:(smp + 1) * QBLOCK]
        else:
            res[grp] = resid
            emit_h(layer + 1, grp, resid)

    @pl.loop(0, n_layers - 1)
    def _(layer):
        @pl.loop(0, n_groups)
        def _(grp):
            step(layer, grp, False)

    @pl.loop(0, n_groups)
    def _(grp):
        step(n_layers - 1, grp, True)

    for direction in range(2):
        mask_copy(direction).wait_send()

    @pl.loop(0, n_layers)
    def _(layer):
        @pl.loop(0, n_groups)
        def _(grp):
            for direction in range(2):
                halo_copy(layer, grp, direction).wait_send()


def solution(mesh):
    n_dev = mesh.shape['sp']

    def device_fn(atom_act, cond, pair, atom_mask, w_cond, b_cond, w_qkvg, b_query, w_pair, w_out, w_up, w_down):
        samples, seq, width = atom_act.shape
        n_layers = w_qkvg.shape[0]
        n_groups = samples // GROUP
        ext = seq + 2 * EDGE
        blocks, _, window, c_pair = pair.shape
        f32, bf16 = jnp.float32, jnp.bfloat16
        pair_t = pair.transpose(0, 1, 3, 2).reshape(blocks * QBLOCK * c_pair, window)
        vmem = pl.BlockSpec(memory_space=pltpu.VMEM)
        hbm = pl.BlockSpec(memory_space=pl.ANY)
        cols = GROUP * seq
        return pl.pallas_call(
            functools.partial(body, n_dev),
            out_shape=jax.ShapeDtypeStruct(atom_act.shape, bf16),
            in_specs=[hbm, vmem, hbm, vmem, hbm, vmem, hbm, vmem, vmem, hbm, hbm, hbm],
            out_specs=vmem,
            scratch_shapes=[
                pltpu.VMEM(atom_act.shape, bf16),
                pltpu.VMEM(pair_t.shape, bf16),
                pltpu.VMEM(w_cond.shape, bf16),
                pltpu.VMEM(w_qkvg.shape, bf16),
                pltpu.VMEM(w_out.shape, bf16),
                pltpu.VMEM(w_up.shape, bf16),
                pltpu.VMEM(w_down.shape, bf16),
                pltpu.VMEM(pair_t.shape, f32),
                pltpu.VMEM((n_groups, width, cols), f32),
                pltpu.VMEM((n_groups, width, cols), bf16),
                pltpu.VMEM((n_layers, samples, ext, width), bf16),
                pltpu.VMEM((n_layers, 6, width, cols), f32),
                pltpu.VMEM((n_layers, GROUP, blocks, KEY_WINDOW, 128), f32),
                pltpu.VMEM((n_layers, width, width), bf16),
                pltpu.VMEM((n_layers, width, width), bf16),
                pltpu.VMEM((n_layers, width, width), bf16),
                pltpu.VMEM((n_layers, 4 * width, width), bf16),
                pltpu.VMEM((n_layers, width, 2 * width), bf16),
                pltpu.VMEM((GROUP, ext, width), bf16),
                pltpu.VMEM((GROUP, cols, width), bf16),
                pltpu.VMEM((GROUP, width, ext), bf16),
                pltpu.VMEM((width, cols), f32),
                pltpu.VMEM((3, 8, 128), jnp.int32),
                pltpu.SemaphoreType.DMA((7,)),
                pltpu.SemaphoreType.DMA((n_layers, n_groups, 2)),
                pltpu.SemaphoreType.DMA((n_layers, n_groups, 2)),
                pltpu.SemaphoreType.DMA((2,)),
                pltpu.SemaphoreType.DMA((2,)),
            ],
            compiler_params=pltpu.CompilerParams(
                collective_id=0, has_side_effects=True, vmem_limit_bytes=60 * 1024 * 1024),
        )(atom_act, cond, pair_t, atom_mask.reshape(1, seq), w_cond, b_cond.reshape(n_layers, 1, 4 * width), w_qkvg, b_query,
          w_pair, w_out, w_up, w_down)

    act_spec = P('dp', 'sp', None)
    in_specs = (act_spec, P('sp', None), P('sp', None, None, None), P('sp'), P(), P(), P(), P(), P(), P(), P(), P())
    return jax.shard_map(device_fn, mesh=mesh, in_specs=in_specs, out_specs=act_spec, check_vma=False)
```

profile of v0, /device:TPU:0, one launch (start us, length us, event | category | flops | bytes accessed | tf_op | source)
XLA Modules:
  0.0 57.4 jit_solution(17655739293222907272)
XLA Ops:
  0.0 1.3 %reshape.11.bcond_ref = f32[3,1,512]{2,1,0:T(1,128)} reshape(f32[3,512]{1,0:T(4,128)} %param.17) | data formatting | bytes 12288 | tf_op jit(solution)/shard_map/reshape | solution.py:321
  1.3 54.2 %shard_map.118 = bf16[32,64,128]{2,1,0:T(8,128)(2,1)} custom-call(bf16[32,64,128]{2,1,0:T(8,128)(2,1)} %act_hbm.1, bf16[64,128]{1,0:T(8,128)(2,1)} %cond_ref.1, bf16[1024,128]{1,0:T(8,128)(2,1)} %bitcast.4, s32[1,64]{1,0:T(1,128)} %bitcast.5, bf16[3,128,768]{2,1,0:T(8,128)(2,1)} %wcond_hbm.1, f32[3,1,512]{2,1,0:T(1,128)} %reshape.11.bcond_ref, ...), custom_call_target="tpu_custom_call" | custom-call | tf_op jit(solution)/shard_map/pallas_call | solution.py:284
  55.5 1.9 %copy.14 = bf16[32,64,128]{2,1,0:T(8,128)(2,1)} copy(bf16[32,64,128]{2,1,0:T(8,128)(2,1)} %shard_map.118) | data formatting | bytes 1048576
where the time goes:
time: 57.7 us; the launch traced here: 57.4 us
  Pallas kernels  54.2 us (94%)
  local copies, waits for them, and re-layouts  3.16 us (5%)
    pallas_call x1, Pallas kernels, device_fn(): pl.pallas_call(functools.partial(body, n_dev), out_shape=jax.ShapeDtypeSt...  54.2 us
    unnamed x1, local copies, waits for them, and re-layouts  1.87 us
    reshape x1, local copies, waits for them, and re-layouts, device_fn(): b_cond.reshape(n_layers, 1, 4 * width)  1.29 us

commit v1 on v0

--- a/solution.py
+++ b/solution.py
@@ -40,8 +40,8 @@
 def body(n_dev, act_hbm, cond_ref, pair_hbm, mask_ref, wcond_hbm, bcond_ref, wqkvg_hbm, bquery_ref, wpair_ref,
          wout_hbm, wup_hbm, wdown_hbm, out_ref,
          act, pair, wcond, wqkvg, wout, wup, wdown,
-         pairf, res, h_cm, h_ext, tab, bias, wv_t, wg_t, wo_t, wu_t, wd_t,
-         k_scr, q_scr, v_scr, o_scr, mask_buf,
+         pairf, res, h_cm, h_ext, tab, bias, wq_t, wg_t, wo_t, wu_t, wd_t, bq_t,
+         k_scr, q_scr, v_scr, o_scr, r_scr, m_scr, mask_buf,
          in_sem, send_sem, recv_sem, msend_sem, mrecv_sem):
     n_layers, width = bquery_ref.shape
     n_heads = width // QBLOCK
@@ -73,7 +73,7 @@
 
     def tables(layer):
         proj = mm(cond_norm, wcond[layer])
-        gates = bcond_ref[layer]
+        gates = bcond_ref[pl.ds(layer, 1), :]
         pieces = []
         for idx, bias_idx in enumerate((0, None, 1, 2, None, 3)):
             piece = proj[:, idx * width:(idx + 1) * width]
@@ -138,7 +138,9 @@
 
     @pl.loop(0, n_layers)
     def _(layer):
-        wv_t[layer] = wqkvg[layer, :, 2 * width:3 * width].T
+        wq_t[layer] = wqkvg[layer, :, :width].T
+        row = jnp.broadcast_to(bquery_ref[pl.ds(layer, 1), :], (width, width)).T
+        bq_t[layer] = jnp.concatenate([row, row], axis=1)
         wg_t[layer] = wqkvg[layer, :, 3 * width:].T
         wo_t[layer] = wout[layer].T
         for idx in range(4):
@@ -179,48 +181,81 @@
                 bias[layer, smp, blk] = table if smp == 0 else pltpu.roll(table, smp * QBLOCK, 1)
 
     lane = lax.broadcasted_iota(jnp.int32, (1, width), 1)
-    head_of_lane = lane // head_dim
     scale = head_dim ** -0.5 * LOG2E
 
-    def step(layer, grp, last):
+    def split(idx):
+        return idx // n_groups, idx % n_groups
+
+    def project(idx):
+        layer, grp = split(idx)
         for direction in range(2):
             halo_copy(layer, grp, direction).wait_recv()
-        w_qk = wqkvg[layer, :, :2 * width]
-        b_q = bquery_ref[pl.ds(layer, 1), :]
-        w_v = wv_t[layer]
+        q_t = mm(wq_t[layer], h_cm[grp])
+        w_kv = wqkvg[layer, :, width:3 * width]
+        yield
         for smp in range(GROUP):
-            h_nat = h_ext[layer, grp * GROUP + smp]
-            q_k = mm(h_nat, w_qk)
-            k_scr[smp] = q_k[:, width:].astype(bf16)
-            q_val = (q_k[EDGE:EDGE + seq, :width] + b_q).astype(bf16)
-            for blk in range(2):
-                rows = q_val[blk * QBLOCK:(blk + 1) * QBLOCK]
-                for slot in range(n_heads):
-                    head = (slot - smp) % n_heads
-                    q_scr[smp, blk * 128 + slot * QBLOCK:blk * 128 + (slot + 1) * QBLOCK, :] = jnp.where(
-                        head_of_lane == head, rows, jnp.zeros_like(rows))
-            v_scr[smp] = mm_nt(w_v, h_nat).astype(bf16)
-        for smp in range(GROUP):
-            logits = mm_nt(k_scr[smp], q_scr[smp])
+            k_v = mm(h_ext[layer, grp * GROUP + smp], w_kv)
+            yield
+            k_scr[smp] = k_v[:, :width].astype(bf16)
+            v_scr[smp] = k_v[:, width:].astype(bf16).T
+            yield
+            if smp == 0:
+                q_t = q_t + bq_t[layer]
+            heads = []
+            for head in range(n_heads):
+                rows = slice(head * head_dim, (head + 1) * head_dim)
+                keep = lane // QBLOCK == (head + smp) % n_heads
+                for blk in range(2):
+                    part = q_t[rows, blk * 128:(blk + 1) * 128]
+                    part = pltpu.roll(part, head * QBLOCK, 1) if head else part
+                    q_scr[smp, rows, blk * 128:(blk + 1) * 128] = jnp.where(keep, part, 0.0).astype(bf16)
+            yield
+
+    def attend(idx):
+        layer, grp = split(idx)
+        logits = {}
+        out = {}
+
+        def score(smp):
+            logits[smp] = mm(k_scr[smp], q_scr[smp])
+
+        def soft(smp):
             probs = []
             for blk in range(2):
-                x = logits[blk * QBLOCK:blk * QBLOCK + KEY_WINDOW, blk * 128:(blk + 1) * 128] * scale + bias[layer, smp, blk]
+                x = logits[smp][blk * QBLOCK:blk * QBLOCK + KEY_WINDOW, blk * 128:(blk + 1) * 128] * scale + bias[layer, smp, blk]
                 e = jnp.exp2(x - jnp.max(x, axis=0, keepdims=True))
                 p = (e * (1.0 / jnp.sum(e, axis=0, keepdims=True))).astype(bf16)
                 zero = jnp.zeros((QBLOCK, 128), bf16)
                 probs.append(jnp.concatenate([zero, p] if blk else [p, zero], axis=0))
-            o_t = mm(v_scr[smp], jnp.concatenate(probs, axis=1))
+            out[smp] = mm(v_scr[smp], jnp.concatenate(probs, axis=1))
+
+        def place(smp):
             for head in range(n_heads):
                 slot = (head + smp) % n_heads
                 rows = slice(head * head_dim, (head + 1) * head_dim)
                 for blk in range(2):
                     cols = slice(blk * 128, (blk + 1) * 128)
-                    part = o_t[rows, cols]
-                    if smp == 0:
-                        o_scr[rows, cols] = part
-                    else:
-                        o_scr[rows, cols] = jnp.where(lane // QBLOCK == slot, part, o_scr[rows, cols])
-        gate = sigmoid(mm(wg_t[layer], h_cm[grp]))
+                    part = out[smp][rows, cols]
+                    if smp:
+                        part = jnp.where(lane // QBLOCK == slot, part, o_scr[rows, cols])
+                    o_scr[rows, cols] = part
+
+        score(0)
+        yield
+        score(1)
+        yield
+        for smp in range(GROUP):
+            soft(smp)
+            yield
+            if smp + 2 < GROUP:
+                score(smp + 2)
+            yield
+            place(smp)
+            yield
+
+    def mix(idx):
+        layer, grp = split(idx)
+        gate = mm(wg_t[layer], h_cm[grp])
         heads = []
         for head in range(n_heads):
             rows = slice(head * head_dim, (head + 1) * head_dim)
@@ -229,32 +264,70 @@
                 part = o_scr[rows, blk * 128:(blk + 1) * 128]
                 parts.append(pltpu.roll(part, (128 - head * QBLOCK) % 128, 1) if head else part)
             heads.append(jnp.concatenate(parts, axis=1))
-        o_val = (gate * jnp.concatenate(heads, axis=0)).astype(bf16)
-        resid = res[grp] + tab[layer, 2] * mm(wo_t[layer], o_val)
+        o_val = (sigmoid(gate) * jnp.concatenate(heads, axis=0)).astype(bf16)
+        proj = mm(wo_t[layer], o_val)
+        yield
+        resid = res[grp] + tab[layer, 2] * proj
+        r_scr[...] = resid
+        yield
         h_t = (norm(resid, 0) * tab[layer, 3] + tab[layer, 4]).astype(bf16)
-        up = mm(wu_t[layer], h_t)
-        left, right = up[:2 * width], up[2 * width:]
-        half = 0.5 * left
-        hidden = ((half * jnp.tanh(half) + half) * right).astype(bf16)
-        resid = resid + tab[layer, 5] * mm(wd_t[layer], hidden)
+        yield
+        n_chunk = 4
+        rows = 2 * width // n_chunk
+        ups = {}
+        for pos in range(n_chunk + 1):
+            if pos < n_chunk:
+                ups[pos] = [mm(wu_t[layer, pl.ds(base + pos * rows, rows), :], h_t) for base in (0, 2 * width)]
+                yield
+            if pos:
+                left, right = ups[pos - 1]
+                half = 0.5 * left
+                m_scr[(pos - 1) * rows:pos * rows, :] = ((half * jnp.tanh(half) + half) * right).astype(bf16)
+                yield
+
+    def finish(idx, last):
+        layer, grp = split(idx)
+        resid = r_scr[...]
+        down = mm(wd_t[layer], m_scr[...])
+        yield
+        resid = resid + tab[layer, 5] * down
+        yield
         if last:
             for blk in range(2):
                 nat = resid[:, blk * 128:(blk + 1) * 128].T.astype(bf16)
                 for smp in range(GROUP):
                     out_ref[grp * GROUP + smp, blk * QBLOCK:(blk + 1) * QBLOCK, :] = nat[smp * QBLOCK:(smp + 1) * QBLOCK]
+                yield
         else:
             res[grp] = resid
+            yield
             emit_h(layer + 1, grp, resid)
-
-    @pl.loop(0, n_layers - 1)
-    def _(layer):
-        @pl.loop(0, n_groups)
-        def _(grp):
-            step(layer, grp, False)
-
-    @pl.loop(0, n_groups)
-    def _(grp):
-        step(n_layers - 1, grp, True)
+            yield
+
+    def interleave(*stages):
+        stages = list(stages)
+        while stages:
+            for stage in list(stages):
+                if next(stage, stages) is stages:
+                    stages.remove(stage)
+
+    n_steps = n_layers * n_groups
+    split_at = n_steps - n_groups
+    interleave(project(0))
+    interleave(attend(0), project(1))
+    interleave(mix(0), attend(1), project(2))
+
+    @pl.loop(2, split_at + 2)
+    def _(idx):
+        interleave(finish(idx - 2, False), mix(idx - 1), attend(idx), project(idx + 1))
+
+    @pl.loop(split_at + 2, n_steps - 1)
+    def _(idx):
+        interleave(finish(idx - 2, True), mix(idx - 1), attend(idx), project(idx + 1))
+
+    interleave(finish(n_steps - 3, True), mix(n_steps - 2), attend(n_steps - 1))
+    interleave(finish(n_steps - 2, True), mix(n_steps - 1))
+    interleave(finish(n_steps - 1, True))
 
     for direction in range(2):
         mask_copy(direction).wait_send()
@@ -305,10 +378,13 @@
                 pltpu.VMEM((n_layers, width, width), bf16),
                 pltpu.VMEM((n_layers, 4 * width, width), bf16),
                 pltpu.VMEM((n_layers, width, 2 * width), bf16),
+                pltpu.VMEM((n_layers, width, cols), f32),
                 pltpu.VMEM((GROUP, ext, width), bf16),
-                pltpu.VMEM((GROUP, cols, width), bf16),
+                pltpu.VMEM((GROUP, width, cols), bf16),
                 pltpu.VMEM((GROUP, width, ext), bf16),
                 pltpu.VMEM((width, cols), f32),
+                pltpu.VMEM((width, cols), f32),
+                pltpu.VMEM((2 * width, cols), bf16),
                 pltpu.VMEM((3, 8, 128), jnp.int32),
                 pltpu.SemaphoreType.DMA((7,)),
                 pltpu.SemaphoreType.DMA((n_layers, n_groups, 2)),
@@ -318,7 +394,7 @@
             ],
             compiler_params=pltpu.CompilerParams(
                 collective_id=0, has_side_effects=True, vmem_limit_bytes=60 * 1024 * 1024),
-        )(atom_act, cond, pair_t, atom_mask.reshape(1, seq), w_cond, b_cond.reshape(n_layers, 1, 4 * width), w_qkvg, b_query,
+        )(atom_act, cond, pair_t, atom_mask.reshape(1, seq), w_cond, b_cond, w_qkvg, b_query,
           w_pair, w_out, w_up, w_down)
 
     act_spec = P('dp', 'sp', None)

time: 57.7 us -> 42.6 us (0.74)
  Pallas kernels: 54.2 us -> 40.5 us
  local copies, waits for them, and re-layouts: 3.16 us -> 1.87 us
    pallas_call x1, Pallas kernels: 54.2 us -> 40.5 us  [device_fn(): pl.pallas_call(functools.partial(body, n_dev), out_shape=jax.ShapeDtypeSt...]
    reshape x1 -> x0, local copies, waits for them, and re-layouts: 1.29 us -> none  [device_fn(): b_cond.reshape(n_layers, 1, 4 * width)]
where the time goes in v1:
time: 42.6 us; the launch traced here: 42.3 us
  Pallas kernels  40.5 us (95%)
  local copies, waits for them, and re-layouts  1.87 us (4%)
    pallas_call x1, Pallas kernels, device_fn(): pl.pallas_call(functools.partial(body, n_dev), out_shape=jax.ShapeDtypeSt...  40.5 us
    unnamed x1, local copies, waits for them, and re-layouts  1.87 us

profile of v1, /device:TPU:0, one launch (start us, length us, event | category | flops | bytes accessed | tf_op | source)
XLA Modules:
  0.0 42.3 jit_solution(17992836897943041266)
XLA Ops:
  0.0 40.5 %shard_map.118 = bf16[32,64,128]{2,1,0:T(8,128)(2,1)} custom-call(bf16[32,64,128]{2,1,0:T(8,128)(2,1)} %act_hbm.1, bf16[64,128]{1,0:T(8,128)(2,1)} %cond_ref.1, bf16[1024,128]{1,0:T(8,128)(2,1)} %bitcast.4, s32[1,64]{1,0:T(1,128)} %bitcast.5, bf16[3,128,768]{2,1,0:T(8,128)(2,1)} %wcond_hbm.1, f32[3,512]{1,0:T(4,128)} %bcond_ref.1, ...), custom_call_target="tpu_custom_call" | custom-call | tf_op jit(solution)/shard_map/pallas_call | solution.py:357
  40.5 1.9 %copy.14 = bf16[32,64,128]{2,1,0:T(8,128)(2,1)} copy(bf16[32,64,128]{2,1,0:T(8,128)(2,1)} %shard_map.118) | data formatting | bytes 1048576

commit v2 on v1

v2 whole, which is shorter than its diff:
```python
import functools
import math

import jax
import jax.numpy as jnp
from jax import lax
from jax.experimental import pallas as pl
from jax.experimental.pallas import tpu as pltpu
from jax.sharding import PartitionSpec as P

QBLOCK = 32
KEY_WINDOW = 128
EDGE = 48
LN_EPS = 1e-5
GROUP = 2
LOG2E = math.log2(math.e)
MESH = pl.DeviceIdType.MESH


def mm(lhs, rhs):
    return jnp.dot(lhs, rhs, preferred_element_type=jnp.float32)


def sigmoid(vals):
    return 0.5 * jnp.tanh(0.5 * vals) + 0.5


def norm(vals, axis):
    mean = jnp.mean(vals, axis=axis, keepdims=True)
    cent = vals - mean
    var = jnp.mean(cent * cent, axis=axis, keepdims=True)
    return cent * lax.rsqrt(var + LN_EPS)


def body(n_dev, act_hbm, cond_hbm, pair_hbm, mask_ref, wcond_hbm, bcond_ref, wqkvg_hbm, bquery_ref, wpair_ref,
         wout_hbm, wup_hbm, wdown_hbm, out_hbm,
         pair, wcond, wqkvg, wout, wup, wdown,
         act_in, cond_in, mask_own, mask_in, bias_own, bias_in, out_stage,
         res, h_cm, h_ext, tab, bias, wq_t, wg_t, wo_t, wu_t, wd_t, bq_t,
         k_scr, q_scr, v_nat, v_scr, o_scr, r_scr, m_scr,
         in_sem, send_sem, recv_sem, csend_sem, crecv_sem, msend_sem, mrecv_sem, asend_sem, arecv_sem,
         bsend_sem, brecv_sem, osend_sem, orecv_sem):
    n_layers, width = bquery_ref.shape
    n_heads = width // QBLOCK
    head_dim = width // n_heads
    samples, seq, _ = act_hbm.shape
    half_smp = samples // 2
    n_groups = half_smp // GROUP
    own = 2 * seq
    ext = own + 2 * EDGE
    n_blocks = own // QBLOCK
    f32, bf16 = jnp.float32, jnp.bfloat16

    me = lax.axis_index('sp')
    plane, row, core = me // 4, (me // 2) % 2, me % 2
    n_planes = n_dev // 4
    chunk = 2 * plane + core
    has_prev, has_next = chunk > 0, chunk < 2 * n_planes - 1

    def owner(chunk_idx, row_idx):
        return (chunk_idx // 2) * 4 + 2 * row_idx + chunk_idx % 2

    def remote(src, dst, ssem, rsem, peer):
        return pltpu.make_async_remote_copy(
            src_ref=src, dst_ref=dst, send_sem=ssem, recv_sem=rsem, device_id={'sp': peer}, device_id_type=MESH)

    def push(src, dst, ssem, rsem, peer):
        @pl.when(peer != me)
        def _():
            remote(src, dst, ssem, rsem, peer).start()

        @pl.when(peer == me)
        def _():
            pltpu.make_async_copy(src, dst, rsem).start()

    def push_done(src, dst, ssem, rsem, peer):
        @pl.when(peer != me)
        def _():
            remote(src, dst, ssem, rsem, peer).wait_send()

    def arrived(dst, rsem):
        pltpu.make_async_copy(dst, dst, rsem).wait()

    loads = [pltpu.make_async_copy(src, dst, in_sem.at[pos]) for pos, (src, dst) in enumerate(
        [(pair_hbm, pair), (wcond_hbm, wcond), (wqkvg_hbm, wqkvg), (wout_hbm, wout), (wup_hbm, wup), (wdown_hbm, wdown)])]
    for load in loads:
        load.start()

    zero_rows = jnp.zeros((GROUP, EDGE, width), bf16)

    @pl.loop(0, n_layers)
    def _(layer):
        @pl.loop(0, n_groups)
        def _(grp):
            h_ext[layer, pl.ds(grp * GROUP, GROUP), 0:EDGE, :] = zero_rows
            h_ext[layer, pl.ds(grp * GROUP, GROUP), EDGE + own:ext, :] = zero_rows

    mask_own[...] = jnp.zeros_like(mask_own)
    mask_own[0:1, 0:seq] = mask_ref[...]
    mask_in[0] = jnp.zeros_like(mask_own)
    mask_in[3] = jnp.zeros_like(mask_own)

    barrier = pltpu.get_barrier_semaphore()

    def greet(plane_idx, skip):
        for other in range(4):
            peer = 4 * plane_idx + other
            if skip:
                @pl.when(peer != me)
                def _():
                    pl.semaphore_signal(barrier, inc=1, device_id={'sp': peer}, device_id_type=MESH)
            else:
                pl.semaphore_signal(barrier, inc=1, device_id={'sp': peer}, device_id_type=MESH)

    greet(plane, True)

    @pl.when(plane > 0)
    def _():
        greet(plane - 1, False)

    @pl.when(plane < n_planes - 1)
    def _():
        greet(plane + 1, False)

    pl.semaphore_wait(barrier, 3 + 4 * jnp.where(plane > 0, 1, 0) + 4 * jnp.where(plane < n_planes - 1, 1, 0))

    home = 2 * plane + row

    def cond_push(half):
        return (cond_hbm, cond_in.at[pl.ds(core * seq, seq)], csend_sem.at[half], crecv_sem.at[core], owner(home, half))

    def mask_push(half):
        return (mask_own, mask_in.at[1 + core], msend_sem.at[half], mrecv_sem.at[1 + core], owner(home, half))

    side = home + 2 * core - 1
    side_slot = 3 - 3 * core
    side_ok = jnp.logical_and(side >= 0, side < 2 * n_planes)

    def mask_side(half):
        return (mask_own, mask_in.at[side_slot], msend_sem.at[2 + half], mrecv_sem.at[side_slot], owner(side, half))

    def act_push(half, grp):
        return (act_hbm.at[pl.ds(half * half_smp + grp * GROUP, GROUP)],
                act_in.at[pl.ds(grp * GROUP, GROUP), pl.ds(core * seq, seq)],
                asend_sem.at[half, grp], arecv_sem.at[core, grp], owner(home, half))

    def bias_push(half, layer):
        return (bias_own.at[layer], bias_in.at[layer, core], bsend_sem.at[half, layer], brecv_sem.at[core, layer],
                owner(home, half))

    for half in range(2):
        push(*cond_push(half))
        push(*mask_push(half))

        @pl.when(side_ok)
        def _():
            push(*mask_side(half))

    early = 3
    for grp in range(early):
        for half in range(2):
            push(*act_push(half, grp))

    c_pair = wpair_ref.shape[0]
    n_col = wpair_ref.shape[1]
    tall, deep = n_col * 16, 16 * c_pair
    pick_col = (lax.broadcasted_iota(jnp.int32, (tall, n_col), 0) // 16
                == lax.broadcasted_iota(jnp.int32, (tall, n_col), 1)).astype(bf16)
    pick_chan = (lax.broadcasted_iota(jnp.int32, (c_pair, deep), 1) % c_pair
                 == lax.broadcasted_iota(jnp.int32, (c_pair, deep), 0)).astype(bf16)
    spread = lax.dot_general(
        wpair_ref[...], pick_chan, (((0,), (0,)), ((), ())), preferred_element_type=f32).astype(bf16)
    spread = mm(pick_col, spread)
    same = (lax.broadcasted_iota(jnp.int32, (tall, deep), 0) % 16 == lax.broadcasted_iota(jnp.int32, (tall, deep), 1) // c_pair)
    w_block = jnp.where(same, spread, 0.0).astype(bf16)
    loads[0].wait()
    for part in range(seq // 16):
        vals = pair[part * deep:(part + 1) * deep].astype(f32).reshape(16, c_pair, KEY_WINDOW)
        vals = norm(vals, 1).astype(bf16).reshape(deep, KEY_WINDOW)
        res_bias = mm(w_block, vals).astype(bf16)
        blk, sub = part // 2, part % 2
        for layer in range(n_layers):
            for head in range(n_heads):
                col = layer * n_heads + head
                bias_own[layer, blk, head * QBLOCK + sub * 16:head * QBLOCK + (sub + 1) * 16, :] = res_bias[col * 16:(col + 1) * 16]
    for half in range(2):
        push(*bias_push(half, 0))
    for grp in range(early, n_groups):
        for half in range(2):
            push(*act_push(half, grp))
    for layer in range(1, n_layers):
        for half in range(2):
            push(*bias_push(half, layer))

    for slot in range(2):
        arrived(cond_in.at[pl.ds(slot * seq, seq)], crecv_sem.at[slot])
    cond_norm = norm(cond_in[...].astype(f32), -1).astype(bf16)
    loads[1].wait()

    def tables(layer):
        proj = mm(cond_norm, wcond[layer])
        gates = bcond_ref[pl.ds(layer, 1), :]
        for idx, bias_idx in enumerate((0, None, 1, 2, None, 3)):
            piece = proj[:, idx * width:(idx + 1) * width]
            if bias_idx is not None:
                piece = sigmoid(piece + gates[:, bias_idx * width:(bias_idx + 1) * width])
            tab[layer, idx] = piece.T

    tables(0)

    def both(vals):
        return jnp.concatenate([vals] * GROUP, axis=1)

    def halo_copy(layer, grp, direction):
        smp = pl.ds(grp * GROUP, GROUP)
        src = pl.ds(own if direction else EDGE, EDGE)
        dst = pl.ds(0 if direction else own + EDGE, EDGE)
        return remote(h_ext.at[layer, smp, src, :], h_ext.at[layer, smp, dst, :],
                      send_sem.at[layer, grp, direction], recv_sem.at[layer, grp, direction],
                      owner(chunk + 1 if direction else chunk - 1, row))

    def halo_start(layer, grp):
        @pl.when(has_prev)
        def _():
            halo_copy(layer, grp, 0).start()

        @pl.when(has_next)
        def _():
            halo_copy(layer, grp, 1).start()

    def halo_wait(layer, grp):
        @pl.when(has_next)
        def _():
            halo_copy(layer, grp, 0).wait_recv()

        @pl.when(has_prev)
        def _():
            halo_copy(layer, grp, 1).wait_recv()

    def emit_h(layer, grp, resid):
        h_t = (norm(resid, 0) * both(tab[layer, 0]) + both(tab[layer, 1])).astype(bf16)
        h_cm[grp] = h_t
        for smp in range(GROUP):
            h_ext[layer, grp * GROUP + smp, EDGE:EDGE + own, :] = h_t[:, smp * own:(smp + 1) * own].T

    def enter(grp):
        for slot in range(2):
            arrived(act_in.at[pl.ds(grp * GROUP, GROUP), pl.ds(slot * seq, seq)], arecv_sem.at[slot, grp])
        cols = [act_in[grp * GROUP + smp].T.astype(f32) for smp in range(GROUP)]
        resid = jnp.concatenate(cols, axis=1)
        res[grp] = resid
        emit_h(0, grp, resid)
        halo_start(0, grp)

    def weights(layer):
        wq_t[layer] = wqkvg[layer, :, :width].T
        bq_t[layer] = jnp.broadcast_to(bquery_ref[pl.ds(layer, 1), :], (width, width)).T
        wg_t[layer] = wqkvg[layer, :, 3 * width:].T
        wo_t[layer] = wout[layer].T
        for idx in range(4):
            wu_t[layer, idx * width:(idx + 1) * width, :] = wup[layer, :, idx * width:(idx + 1) * width].T
        for idx in range(2):
            wd_t[layer, :, idx * width:(idx + 1) * width] = wdown[layer, idx * width:(idx + 1) * width, :].T

    def bias_table(layer, mask_bias):
        for slot in range(2):
            arrived(bias_in.at[layer, slot], brecv_sem.at[slot, layer])
        for blk in range(n_blocks):
            nat = bias_in[layer, blk // 2, blk % 2].astype(f32)
            order = [(slot - blk) % n_heads for slot in range(n_heads)]
            nat = jnp.concatenate([nat[head * QBLOCK:(head + 1) * QBLOCK] for head in order], axis=0)
            bias[layer, blk] = ((nat + mask_bias[:, blk * QBLOCK:blk * QBLOCK + KEY_WINDOW]) * LOG2E).T

    enter(0)
    for load in loads[2:]:
        load.wait()
    weights(0)

    @pl.loop(1, 4)
    def _(grp):
        enter(grp)

    @pl.loop(1, n_layers)
    def _(layer):
        weights(layer)
        tables(layer)

    for slot in range(1, 3):
        arrived(mask_in.at[slot], mrecv_sem.at[slot])

    @pl.when(has_prev)
    def _():
        arrived(mask_in.at[0], mrecv_sem.at[0])

    @pl.when(has_next)
    def _():
        arrived(mask_in.at[3], mrecv_sem.at[3])

    mask_row = jnp.concatenate([mask_in[0, 0:1, seq - EDGE:seq], mask_in[1, 0:1, :seq], mask_in[2, 0:1, :seq],
                                mask_in[3, 0:1, :EDGE], jnp.zeros((1, 256 - ext), jnp.int32)], axis=1)
    mask_bias = (mask_row.astype(f32) - 1.0) * 1e9
    bias_table(0, mask_bias)

    @pl.loop(4, n_groups)
    def _(grp):
        enter(grp)

    for layer in range(1, n_layers):
        bias_table(layer, mask_bias)

    lane = lax.broadcasted_iota(jnp.int32, (1, width), 1)
    scale = head_dim ** -0.5 * LOG2E

    def split(idx):
        return idx // n_groups, idx % n_groups

    def project(idx):
        layer, grp = split(idx)
        q_t = mm(wq_t[layer], h_cm[grp])
        w_kv = wqkvg[layer, :, width:3 * width]
        yield
        for smp in range(GROUP):
            k_v = mm(h_ext[layer, grp * GROUP + smp], w_kv)
            yield
            k_scr[smp] = k_v[:, :width].astype(bf16)
            v_nat[smp] = k_v[:, width:].astype(bf16)
            yield
            if smp == 0:
                q_t = q_t + both(bq_t[layer])
            for head in range(n_heads):
                rows = slice(head * head_dim, (head + 1) * head_dim)
                part = q_t[rows, smp * own:(smp + 1) * own]
                part = pltpu.roll(part, head * QBLOCK, 1) if head else part
                for blk in range(n_blocks):
                    keep = lane // QBLOCK == (head + blk) % n_heads
                    q_scr[smp, rows, blk * 128:(blk + 1) * 128] = jnp.where(keep, part, 0.0).astype(bf16)
                if head % 2:
                    yield
            yield
            v_scr[smp] = v_nat[smp].T
            yield

    def attend(idx):
        layer, grp = split(idx)
        logits = {}
        out = {}

        def score(unit):
            smp, duo = unit // 2, unit % 2
            logits[unit] = mm(k_scr[smp, duo * 64:duo * 64 + 160], q_scr[smp, :, duo * 256:(duo + 1) * 256])

        def soft(unit):
            smp, duo = unit // 2, unit % 2
            probs = []
            for sub in range(2):
                blk = 2 * duo + sub
                x = logits[unit][sub * QBLOCK:sub * QBLOCK + KEY_WINDOW, sub * 128:(sub + 1) * 128] * scale + bias[layer, blk]
                e = jnp.exp2(x - jnp.max(x, axis=0, keepdims=True))
                p = (e * (1.0 / jnp.sum(e, axis=0, keepdims=True))).astype(bf16)
                parts = [p]
                if blk:
                    parts = [jnp.zeros((blk * QBLOCK, 128), bf16)] + parts
                if blk < n_blocks - 1:
                    parts = parts + [jnp.zeros(((n_blocks - 1 - blk) * QBLOCK, 128), bf16)]
                probs.append(jnp.concatenate(parts, axis=0))
            out[unit] = mm(v_scr[smp], jnp.concatenate(probs, axis=1))

        def place(unit):
            smp, duo = unit // 2, unit % 2
            cols = slice(smp * own, (smp + 1) * own)
            for head in range(n_heads):
                rows = slice(head * head_dim, (head + 1) * head_dim)
                for sub in range(2):
                    blk = 2 * duo + sub
                    part = out[unit][rows, sub * 128:(sub + 1) * 128]
                    if blk:
                        part = jnp.where(lane // QBLOCK == (head + blk) % n_heads, part, o_scr[rows, cols])
                    o_scr[rows, cols] = part

        score(0)
        yield
        score(1)
        yield
        for unit in range(2 * GROUP):
            soft(unit)
            yield
            if unit + 2 < 2 * GROUP:
                score(unit + 2)
            yield
            place(unit)
            yield

    def mix(idx):
        layer, grp = split(idx)
        gate = mm(wg_t[layer], h_cm[grp])
        heads = []
        for head in range(n_heads):
            rows = slice(head * head_dim, (head + 1) * head_dim)
            parts = []
            for smp in range(GROUP):
                part = o_scr[rows, smp * own:(smp + 1) * own]
                parts.append(pltpu.roll(part, (128 - head * QBLOCK) % 128, 1) if head else part)
            heads.append(jnp.concatenate(parts, axis=1))
        o_val = (sigmoid(gate) * jnp.concatenate(heads, axis=0)).astype(bf16)
        proj = mm(wo_t[layer], o_val)
        yield
        resid = res[grp] + both(tab[layer, 2]) * proj
        r_scr[...] = resid
        yield
        h_t = (norm(resid, 0) * both(tab[layer, 3]) + both(tab[layer, 4])).astype(bf16)
        yield
        n_chunk = 4
        rows = 2 * width // n_chunk
        ups = {}
        for pos in range(n_chunk + 1):
            if pos < n_chunk:
                ups[pos] = [mm(wu_t[layer, pl.ds(base + pos * rows, rows), :], h_t) for base in (0, 2 * width)]
                yield
            if pos:
                left, right = ups[pos - 1]
                gated = 0.5 * left
                m_scr[(pos - 1) * rows:pos * rows, :] = ((gated * jnp.tanh(gated) + gated) * right).astype(bf16)
                yield

    def finish(idx, last):
        layer, grp = split(idx)
        resid = r_scr[...]
        down = mm(wd_t[layer], m_scr[...])
        yield
        resid = resid + both(tab[layer, 5]) * down
        yield
        if last:
            for smp in range(GROUP):
                out_stage[grp * GROUP + smp] = resid[:, smp * own:(smp + 1) * own].astype(bf16).T
                yield
        else:
            res[grp] = resid
            yield
            emit_h(layer + 1, grp, resid)
            yield

    def out_push(grp, slot):
        return (out_stage.at[pl.ds(grp * GROUP, GROUP), pl.ds(slot * seq, seq)],
                out_hbm.at[pl.ds(row * half_smp + grp * GROUP, GROUP)],
                osend_sem.at[slot, grp], orecv_sem.at[row, grp], 4 * plane + 2 * core + slot)

    def sent(idx, last):
        layer, grp = split(idx)
        if last:
            for slot in range(2):
                push(*out_push(grp, slot))
        else:
            halo_start(layer + 1, grp)

    def interleave(*stages):
        stages = list(stages)
        while stages:
            for stage in list(stages):
                if next(stage, stages) is stages:
                    stages.remove(stage)

    n_steps = n_layers * n_groups
    split_at = n_steps - n_groups
    halo_wait(0, 0)
    interleave(project(0))
    halo_wait(0, 1)
    interleave(attend(0), project(1))
    halo_wait(0, 2)
    interleave(mix(0), attend(1), project(2))

    @pl.loop(2, split_at + 2)
    def _(idx):
        halo_wait(*split(idx + 1))
        interleave(finish(idx - 2, False), mix(idx - 1), attend(idx), project(idx + 1))
        sent(idx - 2, False)

    @pl.loop(split_at + 2, n_steps - 1)
    def _(idx):
        halo_wait(*split(idx + 1))
        interleave(finish(idx - 2, True), mix(idx - 1), attend(idx), project(idx + 1))
        sent(idx - 2, True)

    interleave(finish(n_steps - 3, True), mix(n_steps - 2), attend(n_steps - 1))
    sent(n_steps - 3, True)
    interleave(finish(n_steps - 2, True), mix(n_steps - 1))
    sent(n_steps - 2, True)
    interleave(finish(n_steps - 1, True))
    sent(n_steps - 1, True)

    for half in range(2):
        push_done(*cond_push(half))
        push_done(*mask_push(half))

        @pl.when(side_ok)
        def _():
            push_done(*mask_side(half))

        @pl.loop(0, n_layers)
        def _(layer):
            push_done(*bias_push(half, layer))

        @pl.loop(0, n_groups)
        def _(grp):
            push_done(*act_push(half, grp))
            push_done(*out_push(grp, half))

    @pl.loop(0, n_layers)
    def _(layer):
        @pl.loop(0, n_groups)
        def _(grp):
            @pl.when(has_prev)
            def _():
                halo_copy(layer, grp, 0).wait_send()

            @pl.when(has_next)
            def _():
                halo_copy(layer, grp, 1).wait_send()

    for half in range(2):
        @pl.loop(0, n_groups)
        def _(grp):
            arrived(out_hbm.at[pl.ds(half * half_smp + grp * GROUP, GROUP)], orecv_sem.at[half, grp])


def solution(mesh):
    n_dev = mesh.shape['sp']

    def device_fn(atom_act, cond, pair, atom_mask, w_cond, b_cond, w_qkvg, b_query, w_pair, w_out, w_up, w_down):
        samples, seq, width = atom_act.shape
        n_layers = w_qkvg.shape[0]
        n_heads = width // QBLOCK
        half_smp = samples // 2
        n_groups = half_smp // GROUP
        own = 2 * seq
        ext = own + 2 * EDGE
        n_blocks = own // QBLOCK
        blocks, _, window, c_pair = pair.shape
        f32, bf16 = jnp.float32, jnp.bfloat16
        pair_t = pair.transpose(0, 1, 3, 2).reshape(blocks * QBLOCK * c_pair, window)
        vmem = pl.BlockSpec(memory_space=pltpu.VMEM)
        hbm = pl.BlockSpec(memory_space=pl.ANY)
        cols = GROUP * own
        dma = pltpu.SemaphoreType.DMA
        return pl.pallas_call(
            functools.partial(body, n_dev),
            out_shape=jax.ShapeDtypeStruct(atom_act.shape, bf16),
            in_specs=[hbm, hbm, hbm, vmem, hbm, vmem, hbm, vmem, vmem, hbm, hbm, hbm],
            out_specs=hbm,
            scratch_shapes=[
                pltpu.VMEM(pair_t.shape, bf16),
                pltpu.VMEM(w_cond.shape, bf16),
                pltpu.VMEM(w_qkvg.shape, bf16),
                pltpu.VMEM(w_out.shape, bf16),
                pltpu.VMEM(w_up.shape, bf16),
                pltpu.VMEM(w_down.shape, bf16),
                pltpu.VMEM((half_smp, own, width), bf16),
                pltpu.VMEM((own, width), bf16),
                pltpu.VMEM((8, 128), jnp.int32),
                pltpu.VMEM((4, 8, 128), jnp.int32),
                pltpu.VMEM((n_layers, blocks, n_heads * QBLOCK, window), bf16),
                pltpu.VMEM((n_layers, 2, blocks, n_heads * QBLOCK, window), bf16),
                pltpu.VMEM((half_smp, own, width), bf16),
                pltpu.VMEM((n_groups, width, cols), f32),
                pltpu.VMEM((n_groups, width, cols), bf16),
                pltpu.VMEM((n_layers, half_smp, ext, width), bf16),
                pltpu.VMEM((n_layers, 6, width, own), f32),
                pltpu.VMEM((n_layers, n_blocks, KEY_WINDOW, 128), f32),
                pltpu.VMEM((n_layers, width, width), bf16),
                pltpu.VMEM((n_layers, width, width), bf16),
                pltpu.VMEM((n_layers, width, width), bf16),
                pltpu.VMEM((n_layers, 4 * width, width), bf16),
                pltpu.VMEM((n_layers, width, 2 * width), bf16),
                pltpu.VMEM((n_layers, width, width), f32),
                pltpu.VMEM((GROUP, ext, width), bf16),
                pltpu.VMEM((GROUP, width, n_blocks * 128), bf16),
                pltpu.VMEM((GROUP, ext, width), bf16),
                pltpu.VMEM((GROUP, width, ext), bf16),
                pltpu.VMEM((width, cols), f32),
                pltpu.VMEM((width, cols), f32),
                pltpu.VMEM((2 * width, cols), bf16),
                dma((6,)),
                dma((n_layers, n_groups, 2)),
                dma((n_layers, n_groups, 2)),
                dma((2,)),
                dma((2,)),
                dma((4,)),
                dma((4,)),
                dma((2, n_groups)),
                dma((2, n_groups)),
                dma((2, n_layers)),
                dma((2, n_layers)),
                dma((2, n_groups)),
                dma((2, n_groups)),
            ],
            compiler_params=pltpu.CompilerParams(
                collective_id=0, has_side_effects=True, vmem_limit_bytes=60 * 1024 * 1024),
        )(atom_act, cond, pair_t, atom_mask.reshape(1, seq), w_cond, b_cond, w_qkvg, b_query,
          w_pair, w_out, w_up, w_down)

    act_spec = P('dp', 'sp', None)
    in_specs = (act_spec, P('sp', None), P('sp', None, None, None), P('sp'), P(), P(), P(), P(), P(), P(), P(), P())
    return jax.shard_map(device_fn, mesh=mesh, in_specs=in_specs, out_specs=act_spec, check_vma=False)
```

time: 42.6 us -> 49.1 us (1.15)
  Pallas kernels: 40.5 us -> 47 us
    pallas_call x1, Pallas kernels: 40.5 us -> 47 us  [device_fn(): pl.pallas_call(functools.partial(body, n_dev), out_shape=jax.ShapeDtypeSt...]
where the time goes in v2:
time: 49.1 us; the launch traced here: 48.9 us
  Pallas kernels  47 us (96%)
  local copies, waits for them, and re-layouts  1.87 us (4%)
    pallas_call x1, Pallas kernels, device_fn(): pl.pallas_call(functools.partial(body, n_dev), out_shape=jax.ShapeDtypeSt...  47 us
    unnamed x1, local copies, waits for them, and re-layouts  1.87 us

profile of v2, /device:TPU:0, one launch (start us, length us, event | category | flops | bytes accessed | tf_op | source)
XLA Modules:
  0.0 48.9 jit_solution(865807660436209880)
XLA Ops:
  0.0 47.0 %shard_map.118 = bf16[32,64,128]{2,1,0:T(8,128)(2,1)} custom-call(bf16[32,64,128]{2,1,0:T(8,128)(2,1)} %act_hbm.1, bf16[64,128]{1,0:T(8,128)(2,1)} %cond_hbm.1, bf16[1024,128]{1,0:T(8,128)(2,1)} %bitcast.4, s32[1,64]{1,0:T(1,128)} %bitcast.5, bf16[3,128,768]{2,1,0:T(8,128)(2,1)} %wcond_hbm.1, f32[3,512]{1,0:T(4,128)} %bcond_ref.1, ...), custom_call_target="tpu_custom_call" | custom-call | tf_op jit(solution)/shard_map/pallas_call | solution.py:544
  47.0 1.9 %copy.14 = bf16[32,64,128]{2,1,0:T(8,128)(2,1)} copy(bf16[32,64,128]{2,1,0:T(8,128)(2,1)} %shard_map.118) | data formatting | bytes 1048576

commit v3 on v2

--- a/solution.py
+++ b/solution.py
@@ -37,7 +37,7 @@
          pair, wcond, wqkvg, wout, wup, wdown,
          act_in, cond_in, mask_own, mask_in, bias_own, bias_in, out_stage,
          res, h_cm, h_ext, tab, bias, wq_t, wg_t, wo_t, wu_t, wd_t, bq_t,
-         k_scr, q_scr, v_nat, v_scr, o_scr, r_scr, m_scr,
+         k_scr, q_scr, v_nat, v_scr, o_scr, s_scr, m_scr,
          in_sem, send_sem, recv_sem, csend_sem, crecv_sem, msend_sem, mrecv_sem, asend_sem, arecv_sem,
          bsend_sem, brecv_sem, osend_sem, orecv_sem):
     n_layers, width = bquery_ref.shape
@@ -102,27 +102,19 @@
 
     barrier = pltpu.get_barrier_semaphore()
 
-    def greet(plane_idx, skip):
-        for other in range(4):
-            peer = 4 * plane_idx + other
-            if skip:
-                @pl.when(peer != me)
-                def _():
-                    pl.semaphore_signal(barrier, inc=1, device_id={'sp': peer}, device_id_type=MESH)
-            else:
-                pl.semaphore_signal(barrier, inc=1, device_id={'sp': peer}, device_id_type=MESH)
-
-    greet(plane, True)
-
-    @pl.when(plane > 0)
+    for other in range(4):
+        peer = 4 * plane + other
+
+        @pl.when(peer != me)
+        def _():
+            pl.semaphore_signal(barrier, inc=1, device_id={'sp': peer}, device_id_type=MESH)
+
+    beyond = chunk + 2 * core - 1
+    has_beyond = jnp.logical_and(beyond >= 0, beyond < 2 * n_planes)
+
+    @pl.when(has_beyond)
     def _():
-        greet(plane - 1, False)
-
-    @pl.when(plane < n_planes - 1)
-    def _():
-        greet(plane + 1, False)
-
-    pl.semaphore_wait(barrier, 3 + 4 * jnp.where(plane > 0, 1, 0) + 4 * jnp.where(plane < n_planes - 1, 1, 0))
+        pl.semaphore_signal(barrier, inc=1, device_id={'sp': owner(beyond, row)}, device_id_type=MESH)
 
     home = 2 * plane + row
 
@@ -132,12 +124,9 @@
     def mask_push(half):
         return (mask_own, mask_in.at[1 + core], msend_sem.at[half], mrecv_sem.at[1 + core], owner(home, half))
 
-    side = home + 2 * core - 1
-    side_slot = 3 - 3 * core
-    side_ok = jnp.logical_and(side >= 0, side < 2 * n_planes)
-
-    def mask_side(half):
-        return (mask_own, mask_in.at[side_slot], msend_sem.at[2 + half], mrecv_sem.at[side_slot], owner(side, half))
+    def mask_side(direction):
+        return remote(mask_in.at[1 + direction], mask_in.at[3 - 3 * direction], msend_sem.at[2 + direction],
+                      mrecv_sem.at[3 - 3 * direction], owner(chunk + 2 * direction - 1, row))
 
     def act_push(half, grp):
         return (act_hbm.at[pl.ds(half * half_smp + grp * GROUP, GROUP)],
@@ -147,19 +136,6 @@
     def bias_push(half, layer):
         return (bias_own.at[layer], bias_in.at[layer, core], bsend_sem.at[half, layer], brecv_sem.at[core, layer],
                 owner(home, half))
-
-    for half in range(2):
-        push(*cond_push(half))
-        push(*mask_push(half))
-
-        @pl.when(side_ok)
-        def _():
-            push(*mask_side(half))
-
-    early = 3
-    for grp in range(early):
-        for half in range(2):
-            push(*act_push(half, grp))
 
     c_pair = wpair_ref.shape[0]
     n_col = wpair_ref.shape[1]
@@ -183,75 +159,6 @@
             for head in range(n_heads):
                 col = layer * n_heads + head
                 bias_own[layer, blk, head * QBLOCK + sub * 16:head * QBLOCK + (sub + 1) * 16, :] = res_bias[col * 16:(col + 1) * 16]
-    for half in range(2):
-        push(*bias_push(half, 0))
-    for grp in range(early, n_groups):
-        for half in range(2):
-            push(*act_push(half, grp))
-    for layer in range(1, n_layers):
-        for half in range(2):
-            push(*bias_push(half, layer))
-
-    for slot in range(2):
-        arrived(cond_in.at[pl.ds(slot * seq, seq)], crecv_sem.at[slot])
-    cond_norm = norm(cond_in[...].astype(f32), -1).astype(bf16)
-    loads[1].wait()
-
-    def tables(layer):
-        proj = mm(cond_norm, wcond[layer])
-        gates = bcond_ref[pl.ds(layer, 1), :]
-        for idx, bias_idx in enumerate((0, None, 1, 2, None, 3)):
-            piece = proj[:, idx * width:(idx + 1) * width]
-            if bias_idx is not None:
-                piece = sigmoid(piece + gates[:, bias_idx * width:(bias_idx + 1) * width])
-            tab[layer, idx] = piece.T
-
-    tables(0)
-
-    def both(vals):
-        return jnp.concatenate([vals] * GROUP, axis=1)
-
-    def halo_copy(layer, grp, direction):
-        smp = pl.ds(grp * GROUP, GROUP)
-        src = pl.ds(own if direction else EDGE, EDGE)
-        dst = pl.ds(0 if direction else own + EDGE, EDGE)
-        return remote(h_ext.at[layer, smp, src, :], h_ext.at[layer, smp, dst, :],
-                      send_sem.at[layer, grp, direction], recv_sem.at[layer, grp, direction],
-                      owner(chunk + 1 if direction else chunk - 1, row))
-
-    def halo_start(layer, grp):
-        @pl.when(has_prev)
-        def _():
-            halo_copy(layer, grp, 0).start()
-
-        @pl.when(has_next)
-        def _():
-            halo_copy(layer, grp, 1).start()
-
-    def halo_wait(layer, grp):
-        @pl.when(has_next)
-        def _():
-            halo_copy(layer, grp, 0).wait_recv()
-
-        @pl.when(has_prev)
-        def _():
-            halo_copy(layer, grp, 1).wait_recv()
-
-    def emit_h(layer, grp, resid):
-        h_t = (norm(resid, 0) * both(tab[layer, 0]) + both(tab[layer, 1])).astype(bf16)
-        h_cm[grp] = h_t
-        for smp in range(GROUP):
-            h_ext[layer, grp * GROUP + smp, EDGE:EDGE + own, :] = h_t[:, smp * own:(smp + 1) * own].T
-
-    def enter(grp):
-        for slot in range(2):
-            arrived(act_in.at[pl.ds(grp * GROUP, GROUP), pl.ds(slot * seq, seq)], arecv_sem.at[slot, grp])
-        cols = [act_in[grp * GROUP + smp].T.astype(f32) for smp in range(GROUP)]
-        resid = jnp.concatenate(cols, axis=1)
-        res[grp] = resid
-        emit_h(0, grp, resid)
-        halo_start(0, grp)
-
     def weights(layer):
         wq_t[layer] = wqkvg[layer, :, :width].T
         bq_t[layer] = jnp.broadcast_to(bquery_ref[pl.ds(layer, 1), :], (width, width)).T
@@ -262,32 +169,130 @@
         for idx in range(2):
             wd_t[layer, :, idx * width:(idx + 1) * width] = wdown[layer, idx * width:(idx + 1) * width, :].T
 
-    def bias_table(layer, mask_bias):
+    for load in loads[2:]:
+        load.wait()
+
+    @pl.loop(0, n_layers)
+    def _(layer):
+        weights(layer)
+
+    n_beyond = jnp.where(has_beyond, 1, 0)
+    pl.semaphore_wait(barrier, 3 + n_beyond)
+
+    for half in range(2):
+        push(*cond_push(half))
+    for grp in range(3):
+        for half in range(2):
+            push(*act_push(half, grp))
+        if grp == 0:
+            for half in range(2):
+                push(*mask_push(half))
+    for half in range(2):
+        push(*bias_push(half, 0))
+    for grp in range(3, n_groups):
+        for half in range(2):
+            push(*act_push(half, grp))
+    for layer in range(1, n_layers):
+        for half in range(2):
+            push(*bias_push(half, layer))
+
+    for slot in range(2):
+        arrived(cond_in.at[pl.ds(slot * seq, seq)], crecv_sem.at[slot])
+    cond_norm = norm(cond_in[...].astype(f32), -1).astype(bf16)
+    loads[1].wait()
+
+    def tables(layer):
+        proj = mm(cond_norm, wcond[layer])
+        gates = bcond_ref[pl.ds(layer, 1), :]
+        for idx, bias_idx in enumerate((0, None, 1, 2, None, 3)):
+            piece = proj[:, idx * width:(idx + 1) * width]
+            if bias_idx is not None:
+                piece = sigmoid(piece + gates[:, bias_idx * width:(bias_idx + 1) * width])
+            tab[layer, idx] = piece.T
+
+    def both(vals):
+        return jnp.concatenate([vals] * GROUP, axis=1)
+
+    def halo_copy(layer, grp, direction):
+        smp = pl.ds(grp * GROUP, GROUP)
+        src = pl.ds(own if direction else EDGE, EDGE)
+        dst = pl.ds(0 if direction else own + EDGE, EDGE)
+        return remote(h_ext.at[layer, smp, src, :], h_ext.at[layer, smp, dst, :],
+                      send_sem.at[layer, grp, direction], recv_sem.at[layer, grp, direction],
+                      owner(chunk + 1 if direction else chunk - 1, row))
+
+    def halo_start(layer, grp):
+        @pl.when(has_prev)
+        def _():
+            halo_copy(layer, grp, 0).start()
+
+        @pl.when(has_next)
+        def _():
+            halo_copy(layer, grp, 1).start()
+
+    def halo_wait(layer, grp):
+        @pl.when(has_next)
+        def _():
+            halo_copy(layer, grp, 0).wait_recv()
+
+        @pl.when(has_prev)
+        def _():
+            halo_copy(layer, grp, 1).wait_recv()
+
+    def emit_h(layer, grp, resid):
+        h_t = (norm(resid, 0) * both(tab[layer, 0]) + both(tab[layer, 1])).astype(bf16)
+        h_cm[grp] = h_t
+        for smp in range(GROUP):
+            h_ext[layer, grp * GROUP + smp, EDGE:EDGE + own, :] = h_t[:, smp * own:(smp + 1) * own].T
+
+    def act_wait(grp):
+        for slot in range(2):
+            arrived(act_in.at[pl.ds(grp * GROUP, GROUP), pl.ds(slot * seq, seq)], arecv_sem.at[slot, grp])
+
+    def enter(grp):
+        cols = [act_in[grp * GROUP + smp].T.astype(f32) for smp in range(GROUP)]
+        yield
+        resid = jnp.concatenate(cols, axis=1)
+        res[grp] = resid
+        yield
+        emit_h(0, grp, resid)
+        yield
+
+    def enter_now(grp):
+        act_wait(grp)
+        for _ in enter(grp):
+            pass
+        halo_start(0, grp)
+
+    def bias_wait(layer):
         for slot in range(2):
             arrived(bias_in.at[layer, slot], brecv_sem.at[slot, layer])
+
+    def bias_table(layer, mask_bias):
         for blk in range(n_blocks):
             nat = bias_in[layer, blk // 2, blk % 2].astype(f32)
             order = [(slot - blk) % n_heads for slot in range(n_heads)]
             nat = jnp.concatenate([nat[head * QBLOCK:(head + 1) * QBLOCK] for head in order], axis=0)
             bias[layer, blk] = ((nat + mask_bias[:, blk * QBLOCK:blk * QBLOCK + KEY_WINDOW]) * LOG2E).T
-
-    enter(0)
-    for load in loads[2:]:
-        load.wait()
-    weights(0)
-
-    @pl.loop(1, 4)
-    def _(grp):
-        enter(grp)
-
-    @pl.loop(1, n_layers)
-    def _(layer):
-        weights(layer)
-        tables(layer)
-
+            yield
+
+    tables(0)
+    enter_now(0)
+    tables(1)
+    enter_now(1)
+    tables(2)
     for slot in range(1, 3):
         arrived(mask_in.at[slot], mrecv_sem.at[slot])
 
+    @pl.when(has_prev)
+    def _():
+        mask_side(0).start()
+
+    @pl.when(has_next)
+    def _():
+        mask_side(1).start()
+
+    enter_now(2)
     @pl.when(has_prev)
     def _():
         arrived(mask_in.at[0], mrecv_sem.at[0])
@@ -299,45 +304,55 @@
     mask_row = jnp.concatenate([mask_in[0, 0:1, seq - EDGE:seq], mask_in[1, 0:1, :seq], mask_in[2, 0:1, :seq],
                                 mask_in[3, 0:1, :EDGE], jnp.zeros((1, 256 - ext), jnp.int32)], axis=1)
     mask_bias = (mask_row.astype(f32) - 1.0) * 1e9
-    bias_table(0, mask_bias)
-
-    @pl.loop(4, n_groups)
-    def _(grp):
-        enter(grp)
-
-    for layer in range(1, n_layers):
-        bias_table(layer, mask_bias)
+    bias_wait(0)
+    for _ in bias_table(0, mask_bias):
+        pass
+    enter_now(3)
 
     lane = lax.broadcasted_iota(jnp.int32, (1, width), 1)
     scale = head_dim ** -0.5 * LOG2E
+    keep = [jnp.where(lane // QBLOCK == slot, 1.0, 0.0).astype(bf16) for slot in range(n_heads)]
 
     def split(idx):
         return idx // n_groups, idx % n_groups
 
     def project(idx):
         layer, grp = split(idx)
+        w_kv = wqkvg[layer, :, width:3 * width]
+        k_v = {0: mm(h_ext[layer, grp * GROUP], w_kv)}
+        yield
         q_t = mm(wq_t[layer], h_cm[grp])
-        w_kv = wqkvg[layer, :, width:3 * width]
-        yield
+        yield
+        k_v[1] = mm(h_ext[layer, grp * GROUP + 1], w_kv)
+        yield
+        yield from idle(2)
         for smp in range(GROUP):
-            k_v = mm(h_ext[layer, grp * GROUP + smp], w_kv)
-            yield
-            k_scr[smp] = k_v[:, :width].astype(bf16)
-            v_nat[smp] = k_v[:, width:].astype(bf16)
-            yield
-            if smp == 0:
-                q_t = q_t + both(bq_t[layer])
+            k_scr[smp] = k_v[smp][:, :width].astype(bf16)
+            v_nat[smp] = k_v[smp][:, width:].astype(bf16)
+            yield
             for head in range(n_heads):
                 rows = slice(head * head_dim, (head + 1) * head_dim)
-                part = q_t[rows, smp * own:(smp + 1) * own]
-                part = pltpu.roll(part, head * QBLOCK, 1) if head else part
+                part = q_t[rows, smp * own:(smp + 1) * own] + bq_t[layer, rows]
+                part = (pltpu.roll(part, head * QBLOCK, 1) if head else part).astype(bf16)
                 for blk in range(n_blocks):
-                    keep = lane // QBLOCK == (head + blk) % n_heads
-                    q_scr[smp, rows, blk * 128:(blk + 1) * 128] = jnp.where(keep, part, 0.0).astype(bf16)
+                    q_scr[smp, rows, blk * 128:(blk + 1) * 128] = part * keep[(head + blk) % n_heads]
                 if head % 2:
                     yield
-            yield
             v_scr[smp] = v_nat[smp].T
+            yield
+            if smp == 0:
+                yield from idle(2)
+
+    def score(unit):
+        smp, duo = unit // 2, unit % 2
+        return mm(k_scr[smp, duo * 64:duo * 64 + 160], q_scr[smp, :, duo * 256:(duo + 1) * 256])
+
+    def score_early():
+        for unit in range(2):
+            logit = score(unit)
+            yield
+            for sub in range(2):
+                s_scr[unit, sub] = logit[sub * QBLOCK:sub * QBLOCK + KEY_WINDOW, sub * 128:(sub + 1) * 128]
             yield
 
     def attend(idx):
@@ -345,54 +360,55 @@
         logits = {}
         out = {}
 
-        def score(unit):
-            smp, duo = unit // 2, unit % 2
-            logits[unit] = mm(k_scr[smp, duo * 64:duo * 64 + 160], q_scr[smp, :, duo * 256:(duo + 1) * 256])
-
-        def soft(unit):
-            smp, duo = unit // 2, unit % 2
-            probs = []
-            for sub in range(2):
-                blk = 2 * duo + sub
-                x = logits[unit][sub * QBLOCK:sub * QBLOCK + KEY_WINDOW, sub * 128:(sub + 1) * 128] * scale + bias[layer, blk]
-                e = jnp.exp2(x - jnp.max(x, axis=0, keepdims=True))
-                p = (e * (1.0 / jnp.sum(e, axis=0, keepdims=True))).astype(bf16)
-                parts = [p]
-                if blk:
-                    parts = [jnp.zeros((blk * QBLOCK, 128), bf16)] + parts
-                if blk < n_blocks - 1:
-                    parts = parts + [jnp.zeros(((n_blocks - 1 - blk) * QBLOCK, 128), bf16)]
-                probs.append(jnp.concatenate(parts, axis=0))
-            out[unit] = mm(v_scr[smp], jnp.concatenate(probs, axis=1))
+        def prob(unit, sub):
+            blk = 2 * (unit % 2) + sub
+            if unit < 2:
+                x = s_scr[unit, sub]
+            else:
+                x = logits[unit][sub * QBLOCK:sub * QBLOCK + KEY_WINDOW, sub * 128:(sub + 1) * 128]
+            x = x * scale + bias[layer, blk]
+            e = jnp.exp2(x - jnp.max(x, axis=0, keepdims=True))
+            p = (e * (1.0 / jnp.sum(e, axis=0, keepdims=True))).astype(bf16)
+            parts = [p]
+            if blk:
+                parts = [jnp.zeros((blk * QBLOCK, 128), bf16)] + parts
+            if blk < n_blocks - 1:
+                parts = parts + [jnp.zeros(((n_blocks - 1 - blk) * QBLOCK, 128), bf16)]
+            return jnp.concatenate(parts, axis=0)
 
         def place(unit):
             smp, duo = unit // 2, unit % 2
             cols = slice(smp * own, (smp + 1) * own)
             for head in range(n_heads):
                 rows = slice(head * head_dim, (head + 1) * head_dim)
-                for sub in range(2):
-                    blk = 2 * duo + sub
-                    part = out[unit][rows, sub * 128:(sub + 1) * 128]
-                    if blk:
-                        part = jnp.where(lane // QBLOCK == (head + blk) % n_heads, part, o_scr[rows, cols])
-                    o_scr[rows, cols] = part
-
-        score(0)
-        yield
-        score(1)
-        yield
+                pair_out = [out[unit][rows, sub * 128:(sub + 1) * 128] for sub in range(2)]
+                pick = lane // QBLOCK == (head + 2 * duo + 1) % n_heads
+                merged = jnp.where(pick, pair_out[1], pair_out[0])
+                if duo:
+                    first = lane // QBLOCK == (head + 2) % n_heads
+                    merged = jnp.where(jnp.logical_or(pick, first), merged, o_scr[rows, cols])
+                o_scr[rows, cols] = merged
+
         for unit in range(2 * GROUP):
-            soft(unit)
-            yield
-            if unit + 2 < 2 * GROUP:
-                score(unit + 2)
-            yield
-            place(unit)
-            yield
+            if unit >= 2:
+                logits[unit] = score(unit) if unit not in logits else logits[unit]
+            probs = []
+            for sub in range(2):
+                probs.append(prob(unit, sub))
+                yield
+            out[unit] = mm(v_scr[unit // 2], jnp.concatenate(probs, axis=1))
+            if unit + 2 < 2 * GROUP and unit + 2 >= 2:
+                logits[unit + 2] = score(unit + 2)
+            if unit:
+                place(unit - 1)
+            yield
+        place(2 * GROUP - 1)
+        yield
 
     def mix(idx):
         layer, grp = split(idx)
         gate = mm(wg_t[layer], h_cm[grp])
+        yield
         heads = []
         for head in range(n_heads):
             rows = slice(head * head_dim, (head + 1) * head_dim)
@@ -404,8 +420,9 @@
         o_val = (sigmoid(gate) * jnp.concatenate(heads, axis=0)).astype(bf16)
         proj = mm(wo_t[layer], o_val)
         yield
+        yield from idle(2)
         resid = res[grp] + both(tab[layer, 2]) * proj
-        r_scr[...] = resid
+        res[grp] = resid
         yield
         h_t = (norm(resid, 0) * both(tab[layer, 3]) + both(tab[layer, 4])).astype(bf16)
         yield
@@ -416,6 +433,8 @@
             if pos < n_chunk:
                 ups[pos] = [mm(wu_t[layer, pl.ds(base + pos * rows, rows), :], h_t) for base in (0, 2 * width)]
                 yield
+                if pos == 0:
+                    yield from idle(0)
             if pos:
                 left, right = ups[pos - 1]
                 gated = 0.5 * left
@@ -424,10 +443,10 @@
 
     def finish(idx, last):
         layer, grp = split(idx)
-        resid = r_scr[...]
         down = mm(wd_t[layer], m_scr[...])
         yield
-        resid = resid + both(tab[layer, 5]) * down
+        yield from idle(2)
+        resid = res[grp] + both(tab[layer, 5]) * down
         yield
         if last:
             for smp in range(GROUP):
@@ -452,6 +471,14 @@
         else:
             halo_start(layer + 1, grp)
 
+    def idle(rounds):
+        for _ in range(rounds):
+            yield
+
+    def chain(*parts):
+        for part in parts:
+            yield from part
+
     def interleave(*stages):
         stages = list(stages)
         while stages:
@@ -459,26 +486,49 @@
                 if next(stage, stages) is stages:
                     stages.remove(stage)
 
+    def loop_body(idx, last, *extra):
+        halo_wait(*split(idx + 1))
+        interleave(
+            attend(idx),
+            chain(idle(7), finish(idx - 2, last)),
+            chain(idle(1), mix(idx - 1)),
+            chain(project(idx + 1), idle(1), score_early()), *extra)
+        sent(idx - 2, last)
+
     n_steps = n_layers * n_groups
     split_at = n_steps - n_groups
+    act_wait(4)
     halo_wait(0, 0)
-    interleave(project(0))
+    interleave(enter(4), chain(project(0), score_early()))
+    halo_start(0, 4)
+    act_wait(5)
     halo_wait(0, 1)
-    interleave(attend(0), project(1))
+    interleave(attend(0), chain(project(1), idle(1), score_early()), enter(5))
+    halo_start(0, 5)
+    act_wait(6)
     halo_wait(0, 2)
-    interleave(mix(0), attend(1), project(2))
-
-    @pl.loop(2, split_at + 2)
+    interleave(mix(0), attend(1), chain(project(2), idle(1), score_early()), enter(6))
+    halo_start(0, 6)
+    act_wait(7)
+    loop_body(2, False, enter(7))
+    halo_start(0, 7)
+
+    @pl.loop(3, 6)
     def _(idx):
-        halo_wait(*split(idx + 1))
-        interleave(finish(idx - 2, False), mix(idx - 1), attend(idx), project(idx + 1))
-        sent(idx - 2, False)
+        loop_body(idx, False)
+
+    @pl.loop(6, 8)
+    def _(idx):
+        bias_wait(idx - 5)
+        loop_body(idx, False, bias_table(idx - 5, mask_bias))
+
+    @pl.loop(8, split_at + 2)
+    def _(idx):
+        loop_body(idx, False)
 
     @pl.loop(split_at + 2, n_steps - 1)
     def _(idx):
-        halo_wait(*split(idx + 1))
-        interleave(finish(idx - 2, True), mix(idx - 1), attend(idx), project(idx + 1))
-        sent(idx - 2, True)
+        loop_body(idx, True)
 
     interleave(finish(n_steps - 3, True), mix(n_steps - 2), attend(n_steps - 1))
     sent(n_steps - 3, True)
@@ -491,10 +541,6 @@
         push_done(*cond_push(half))
         push_done(*mask_push(half))
 
-        @pl.when(side_ok)
-        def _():
-            push_done(*mask_side(half))
-
         @pl.loop(0, n_layers)
         def _(layer):
             push_done(*bias_push(half, layer))
@@ -503,6 +549,14 @@
         def _(grp):
             push_done(*act_push(half, grp))
             push_done(*out_push(grp, half))
+
+    @pl.when(has_prev)
+    def _():
+        mask_side(0).wait_send()
+
+    @pl.when(has_next)
+    def _():
+        mask_side(1).wait_send()
 
     @pl.loop(0, n_layers)
     def _(layer):
@@ -576,7 +630,7 @@
                 pltpu.VMEM((GROUP, ext, width), bf16),
                 pltpu.VMEM((GROUP, width, ext), bf16),
                 pltpu.VMEM((width, cols), f32),
-                pltpu.VMEM((width, cols), f32),
+                pltpu.VMEM((2, 2, KEY_WINDOW, 128), f32),
                 pltpu.VMEM((2 * width, cols), bf16),
                 dma((6,)),
                 dma((n_layers, n_groups, 2)),

time: 49.1 us -> 40 us (0.81)
  Pallas kernels: 47 us -> 37.8 us
    pallas_call x1, Pallas kernels: 47 us -> 37.8 us  [device_fn(): pl.pallas_call(functools.partial(body, n_dev), out_shape=jax.ShapeDtypeSt...]
where the time goes in v3:
time: 40 us; the launch traced here: 39.6 us
  Pallas kernels  37.8 us (94%)
  local copies, waits for them, and re-layouts  1.87 us (5%)
    pallas_call x1, Pallas kernels, device_fn(): pl.pallas_call(functools.partial(body, n_dev), out_shape=jax.ShapeDtypeSt...  37.8 us
    unnamed x1, local copies, waits for them, and re-layouts  1.87 us

profile of v3, /device:TPU:0, one launch (start us, length us, event | category | flops | bytes accessed | tf_op | source)
XLA Modules:
  0.0 39.6 jit_solution(14453383891240266760)
XLA Ops:
  0.0 37.8 %shard_map.118 = bf16[32,64,128]{2,1,0:T(8,128)(2,1)} custom-call(bf16[32,64,128]{2,1,0:T(8,128)(2,1)} %act_hbm.1, bf16[64,128]{1,0:T(8,128)(2,1)} %cond_hbm.1, bf16[1024,128]{1,0:T(8,128)(2,1)} %bitcast.4, s32[1,64]{1,0:T(1,128)} %bitcast.5, bf16[3,128,768]{2,1,0:T(8,128)(2,1)} %wcond_hbm.1, f32[3,512]{1,0:T(4,128)} %bcond_ref.1, ...), custom_call_target="tpu_custom_call" | custom-call | tf_op jit(solution)/shard_map/pallas_call | solution.py:598
  37.8 1.9 %copy.14 = bf16[32,64,128]{2,1,0:T(8,128)(2,1)} copy(bf16[32,64,128]{2,1,0:T(8,128)(2,1)} %shard_map.118) | data formatting | bytes 1048576

commit v4 on v3

--- a/solution.py
+++ b/solution.py
@@ -21,6 +21,10 @@
     return jnp.dot(lhs, rhs, preferred_element_type=jnp.float32)
 
 
+def mm_nt(lhs, rhs):
+    return lax.dot_general(lhs, rhs, (((1,), (1,)), ((), ())), preferred_element_type=jnp.float32)
+
+
 def sigmoid(vals):
     return 0.5 * jnp.tanh(0.5 * vals) + 0.5
 
@@ -34,10 +38,10 @@
 
 def body(n_dev, act_hbm, cond_hbm, pair_hbm, mask_ref, wcond_hbm, bcond_ref, wqkvg_hbm, bquery_ref, wpair_ref,
          wout_hbm, wup_hbm, wdown_hbm, out_hbm,
-         pair, wcond, wqkvg, wout, wup, wdown,
+         pair, wcond, wqkvg, wout, wup, wdown, cond_own, act,
          act_in, cond_in, mask_own, mask_in, bias_own, bias_in, out_stage,
-         res, h_cm, h_ext, tab, bias, wq_t, wg_t, wo_t, wu_t, wd_t, bq_t,
-         k_scr, q_scr, v_nat, v_scr, o_scr, s_scr, m_scr,
+         res, h_cm, h_ext, tab, bias, wv_t, wg_t, wo_t, wu_t, wd_t,
+         k_scr, q_scr, v_scr, o_scr, s_scr, m_scr, h_mid,
          in_sem, send_sem, recv_sem, csend_sem, crecv_sem, msend_sem, mrecv_sem, asend_sem, arecv_sem,
          bsend_sem, brecv_sem, osend_sem, orecv_sem):
     n_layers, width = bquery_ref.shape
@@ -82,7 +86,8 @@
         pltpu.make_async_copy(dst, dst, rsem).wait()
 
     loads = [pltpu.make_async_copy(src, dst, in_sem.at[pos]) for pos, (src, dst) in enumerate(
-        [(pair_hbm, pair), (wcond_hbm, wcond), (wqkvg_hbm, wqkvg), (wout_hbm, wout), (wup_hbm, wup), (wdown_hbm, wdown)])]
+        [(pair_hbm, pair), (wcond_hbm, wcond), (wqkvg_hbm, wqkvg), (wout_hbm, wout), (wup_hbm, wup), (wdown_hbm, wdown),
+         (cond_hbm, cond_own), (act_hbm, act)])]
     for load in loads:
         load.start()
 
@@ -118,24 +123,24 @@
 
     home = 2 * plane + row
 
-    def cond_push(half):
-        return (cond_hbm, cond_in.at[pl.ds(core * seq, seq)], csend_sem.at[half], crecv_sem.at[core], owner(home, half))
-
-    def mask_push(half):
-        return (mask_own, mask_in.at[1 + core], msend_sem.at[half], mrecv_sem.at[1 + core], owner(home, half))
+    def cond_push(dest):
+        return (cond_own, cond_in.at[pl.ds(core * seq, seq)], csend_sem.at[dest], crecv_sem.at[core], owner(home, dest))
+
+    def mask_push(dest):
+        return (mask_own, mask_in.at[1 + core], msend_sem.at[dest], mrecv_sem.at[1 + core], owner(home, dest))
 
     def mask_side(direction):
         return remote(mask_in.at[1 + direction], mask_in.at[3 - 3 * direction], msend_sem.at[2 + direction],
                       mrecv_sem.at[3 - 3 * direction], owner(chunk + 2 * direction - 1, row))
 
-    def act_push(half, grp):
-        return (act_hbm.at[pl.ds(half * half_smp + grp * GROUP, GROUP)],
+    def act_push(dest, grp):
+        return (act.at[pl.ds(dest * half_smp + grp * GROUP, GROUP)],
                 act_in.at[pl.ds(grp * GROUP, GROUP), pl.ds(core * seq, seq)],
-                asend_sem.at[half, grp], arecv_sem.at[core, grp], owner(home, half))
-
-    def bias_push(half, layer):
-        return (bias_own.at[layer], bias_in.at[layer, core], bsend_sem.at[half, layer], brecv_sem.at[core, layer],
-                owner(home, half))
+                asend_sem.at[dest], arecv_sem.at[core, grp], owner(home, dest))
+
+    def bias_push(dest, layer):
+        return (bias_own.at[layer], bias_in.at[layer, core], bsend_sem.at[dest], brecv_sem.at[core, layer],
+                owner(home, dest))
 
     c_pair = wpair_ref.shape[0]
     n_col = wpair_ref.shape[1]
@@ -159,13 +164,15 @@
             for head in range(n_heads):
                 col = layer * n_heads + head
                 bias_own[layer, blk, head * QBLOCK + sub * 16:head * QBLOCK + (sub + 1) * 16, :] = res_bias[col * 16:(col + 1) * 16]
+    half = jnp.array(0.5, bf16)
+
     def weights(layer):
-        wq_t[layer] = wqkvg[layer, :, :width].T
-        bq_t[layer] = jnp.broadcast_to(bquery_ref[pl.ds(layer, 1), :], (width, width)).T
-        wg_t[layer] = wqkvg[layer, :, 3 * width:].T
+        wv_t[layer] = wqkvg[layer, :, 2 * width:3 * width].T
+        wg_t[layer] = wqkvg[layer, :, 3 * width:].T * half
         wo_t[layer] = wout[layer].T
         for idx in range(4):
-            wu_t[layer, idx * width:(idx + 1) * width, :] = wup[layer, :, idx * width:(idx + 1) * width].T
+            piece = wup[layer, :, idx * width:(idx + 1) * width].T
+            wu_t[layer, idx * width:(idx + 1) * width, :] = piece * half if idx < 2 else piece
         for idx in range(2):
             wd_t[layer, :, idx * width:(idx + 1) * width] = wdown[layer, idx * width:(idx + 1) * width, :].T
 
@@ -179,33 +186,33 @@
     n_beyond = jnp.where(has_beyond, 1, 0)
     pl.semaphore_wait(barrier, 3 + n_beyond)
 
-    for half in range(2):
-        push(*cond_push(half))
+    for dest in range(2):
+        push(*cond_push(dest))
     for grp in range(3):
-        for half in range(2):
-            push(*act_push(half, grp))
+        for dest in range(2):
+            push(*act_push(dest, grp))
         if grp == 0:
-            for half in range(2):
-                push(*mask_push(half))
-    for half in range(2):
-        push(*bias_push(half, 0))
+            for dest in range(2):
+                push(*mask_push(dest))
+    for dest in range(2):
+        push(*bias_push(dest, 0))
     for grp in range(3, n_groups):
-        for half in range(2):
-            push(*act_push(half, grp))
+        for dest in range(2):
+            push(*act_push(dest, grp))
     for layer in range(1, n_layers):
-        for half in range(2):
-            push(*bias_push(half, layer))
+        for dest in range(2):
+            push(*bias_push(dest, layer))
 
     for slot in range(2):
         arrived(cond_in.at[pl.ds(slot * seq, seq)], crecv_sem.at[slot])
     cond_norm = norm(cond_in[...].astype(f32), -1).astype(bf16)
     loads[1].wait()
 
-    def tables(layer):
-        proj = mm(cond_norm, wcond[layer])
+    def tables(layer, first=0, last=6):
+        proj = mm(cond_norm, wcond[layer, :, first * width:last * width])
         gates = bcond_ref[pl.ds(layer, 1), :]
-        for idx, bias_idx in enumerate((0, None, 1, 2, None, 3)):
-            piece = proj[:, idx * width:(idx + 1) * width]
+        for idx, bias_idx in list(enumerate((0, None, 1, 2, None, 3)))[first:last]:
+            piece = proj[:, (idx - first) * width:(idx - first + 1) * width]
             if bias_idx is not None:
                 piece = sigmoid(piece + gates[:, bias_idx * width:(bias_idx + 1) * width])
             tab[layer, idx] = piece.T
@@ -218,7 +225,7 @@
         src = pl.ds(own if direction else EDGE, EDGE)
         dst = pl.ds(0 if direction else own + EDGE, EDGE)
         return remote(h_ext.at[layer, smp, src, :], h_ext.at[layer, smp, dst, :],
-                      send_sem.at[layer, grp, direction], recv_sem.at[layer, grp, direction],
+                      send_sem.at[direction], recv_sem.at[layer, grp, direction],
                       owner(chunk + 1 if direction else chunk - 1, row))
 
     def halo_start(layer, grp):
@@ -276,8 +283,9 @@
             bias[layer, blk] = ((nat + mask_bias[:, blk * QBLOCK:blk * QBLOCK + KEY_WINDOW]) * LOG2E).T
             yield
 
-    tables(0)
+    tables(0, 0, 2)
     enter_now(0)
+    tables(0, 2, 6)
     tables(1)
     enter_now(1)
     tables(2)
@@ -318,34 +326,56 @@
 
     def project(idx):
         layer, grp = split(idx)
-        w_kv = wqkvg[layer, :, width:3 * width]
-        k_v = {0: mm(h_ext[layer, grp * GROUP], w_kv)}
-        yield
-        q_t = mm(wq_t[layer], h_cm[grp])
-        yield
-        k_v[1] = mm(h_ext[layer, grp * GROUP + 1], w_kv)
-        yield
+        w_qk = wqkvg[layer, :, :2 * width]
+        b_q = bquery_ref[pl.ds(layer, 1), :]
+        q_k = {}
+        v_t = {}
+
+        def k_q(smp):
+            q_k[smp] = mm(h_ext[layer, grp * GROUP + smp], w_qk)
+
+        def vals(smp):
+            v_t[smp] = mm_nt(wv_t[layer], h_ext[layer, grp * GROUP + smp])
+
+        def keys(smp):
+            k_scr[smp] = q_k[smp][:, width:].astype(bf16)
+
+        def queries(smp):
+            q_val = (q_k[smp][EDGE:EDGE + own, :width] + b_q).astype(bf16)
+            for blk in range(n_blocks):
+                part = q_val[blk * QBLOCK:(blk + 1) * QBLOCK]
+                for slot in range(n_heads):
+                    first = blk * 128 + slot * QBLOCK
+                    q_scr[smp, first:first + QBLOCK, :] = part * keep[(slot - blk) % n_heads]
+                if blk % 2:
+                    yield
+
+        k_q(0)
+        yield
+        yield from idle(0)
+        vals(0)
+        yield
+        yield from idle(0)
+        keys(0)
+        yield
+        yield from queries(0)
+        k_q(1)
+        yield from idle(0)
+        v_scr[0] = v_t[0].astype(bf16)
+        yield
+        vals(1)
+        yield
+        yield from idle(0)
+        keys(1)
+        yield
+        yield from queries(1)
         yield from idle(2)
-        for smp in range(GROUP):
-            k_scr[smp] = k_v[smp][:, :width].astype(bf16)
-            v_nat[smp] = k_v[smp][:, width:].astype(bf16)
-            yield
-            for head in range(n_heads):
-                rows = slice(head * head_dim, (head + 1) * head_dim)
-                part = q_t[rows, smp * own:(smp + 1) * own] + bq_t[layer, rows]
-                part = (pltpu.roll(part, head * QBLOCK, 1) if head else part).astype(bf16)
-                for blk in range(n_blocks):
-                    q_scr[smp, rows, blk * 128:(blk + 1) * 128] = part * keep[(head + blk) % n_heads]
-                if head % 2:
-                    yield
-            v_scr[smp] = v_nat[smp].T
-            yield
-            if smp == 0:
-                yield from idle(2)
+        v_scr[1] = v_t[1].astype(bf16)
+        yield
 
     def score(unit):
         smp, duo = unit // 2, unit % 2
-        return mm(k_scr[smp, duo * 64:duo * 64 + 160], q_scr[smp, :, duo * 256:(duo + 1) * 256])
+        return mm_nt(k_scr[smp, duo * 64:duo * 64 + 160], q_scr[smp, duo * 256:(duo + 1) * 256, :])
 
     def score_early():
         for unit in range(2):
@@ -368,7 +398,7 @@
                 x = logits[unit][sub * QBLOCK:sub * QBLOCK + KEY_WINDOW, sub * 128:(sub + 1) * 128]
             x = x * scale + bias[layer, blk]
             e = jnp.exp2(x - jnp.max(x, axis=0, keepdims=True))
-            p = (e * (1.0 / jnp.sum(e, axis=0, keepdims=True))).astype(bf16)
+            p = (e * (0.5 / jnp.sum(e, axis=0, keepdims=True))).astype(bf16)
             parts = [p]
             if blk:
                 parts = [jnp.zeros((blk * QBLOCK, 128), bf16)] + parts
@@ -409,6 +439,7 @@
         layer, grp = split(idx)
         gate = mm(wg_t[layer], h_cm[grp])
         yield
+        yield from idle(2)
         heads = []
         for head in range(n_heads):
             rows = slice(head * head_dim, (head + 1) * head_dim)
@@ -417,16 +448,21 @@
                 part = o_scr[rows, smp * own:(smp + 1) * own]
                 parts.append(pltpu.roll(part, (128 - head * QBLOCK) % 128, 1) if head else part)
             heads.append(jnp.concatenate(parts, axis=1))
-        o_val = (sigmoid(gate) * jnp.concatenate(heads, axis=0)).astype(bf16)
+        o_val = ((jnp.tanh(gate) + 1.0) * jnp.concatenate(heads, axis=0)).astype(bf16)
         proj = mm(wo_t[layer], o_val)
         yield
         yield from idle(2)
         resid = res[grp] + both(tab[layer, 2]) * proj
         res[grp] = resid
         yield
-        h_t = (norm(resid, 0) * both(tab[layer, 3]) + both(tab[layer, 4])).astype(bf16)
-        yield
-        n_chunk = 4
+        yield from idle(4)
+        h_mid[...] = (norm(resid, 0) * both(tab[layer, 3]) + both(tab[layer, 4])).astype(bf16)
+        yield
+
+    def finish(idx, last):
+        layer, grp = split(idx)
+        h_t = h_mid[...]
+        n_chunk = 2
         rows = 2 * width // n_chunk
         ups = {}
         for pos in range(n_chunk + 1):
@@ -434,18 +470,14 @@
                 ups[pos] = [mm(wu_t[layer, pl.ds(base + pos * rows, rows), :], h_t) for base in (0, 2 * width)]
                 yield
                 if pos == 0:
-                    yield from idle(0)
+                    yield from idle(1)
             if pos:
                 left, right = ups[pos - 1]
-                gated = 0.5 * left
-                m_scr[(pos - 1) * rows:pos * rows, :] = ((gated * jnp.tanh(gated) + gated) * right).astype(bf16)
+                m_scr[(pos - 1) * rows:pos * rows, :] = ((left * jnp.tanh(left) + left) * right).astype(bf16)
                 yield
-
-    def finish(idx, last):
-        layer, grp = split(idx)
         down = mm(wd_t[layer], m_scr[...])
         yield
-        yield from idle(2)
+        yield from idle(0)
         resid = res[grp] + both(tab[layer, 5]) * down
         yield
         if last:
@@ -461,7 +493,7 @@
     def out_push(grp, slot):
         return (out_stage.at[pl.ds(grp * GROUP, GROUP), pl.ds(slot * seq, seq)],
                 out_hbm.at[pl.ds(row * half_smp + grp * GROUP, GROUP)],
-                osend_sem.at[slot, grp], orecv_sem.at[row, grp], 4 * plane + 2 * core + slot)
+                osend_sem.at[slot], orecv_sem.at[row], 4 * plane + 2 * core + slot)
 
     def sent(idx, last):
         layer, grp = split(idx)
@@ -488,11 +520,7 @@
 
     def loop_body(idx, last, *extra):
         halo_wait(*split(idx + 1))
-        interleave(
-            attend(idx),
-            chain(idle(7), finish(idx - 2, last)),
-            chain(idle(1), mix(idx - 1)),
-            chain(project(idx + 1), idle(1), score_early()), *extra)
+        interleave(chain(idle(1), finish(idx - 2, last)), chain(idle(0), mix(idx - 1)), attend(idx), chain(idle(2), project(idx + 1)), chain(idle(10), score_early()), *extra)
         sent(idx - 2, last)
 
     n_steps = n_layers * n_groups
@@ -503,11 +531,11 @@
     halo_start(0, 4)
     act_wait(5)
     halo_wait(0, 1)
-    interleave(attend(0), chain(project(1), idle(1), score_early()), enter(5))
+    interleave(attend(0), chain(project(1), score_early()), enter(5))
     halo_start(0, 5)
     act_wait(6)
     halo_wait(0, 2)
-    interleave(mix(0), attend(1), chain(project(2), idle(1), score_early()), enter(6))
+    interleave(mix(0), attend(1), chain(project(2), score_early()), enter(6))
     halo_start(0, 6)
     act_wait(7)
     loop_body(2, False, enter(7))
@@ -537,43 +565,34 @@
     interleave(finish(n_steps - 1, True))
     sent(n_steps - 1, True)
 
-    for half in range(2):
-        push_done(*cond_push(half))
-        push_done(*mask_push(half))
-
-        @pl.loop(0, n_layers)
-        def _(layer):
-            push_done(*bias_push(half, layer))
-
-        @pl.loop(0, n_groups)
-        def _(grp):
-            push_done(*act_push(half, grp))
-            push_done(*out_push(grp, half))
+    def drained(src, ssem):
+        pltpu.make_async_copy(src, src, ssem).wait()
+
+    for dest in range(2):
+        push_done(*cond_push(dest))
+        push_done(*mask_push(dest))
+
+        @pl.when(owner(home, dest) != me)
+        def _():
+            drained(bias_own, bsend_sem.at[dest])
+            drained(act.at[pl.ds(0, half_smp)], asend_sem.at[dest])
+
+        @pl.when(4 * plane + 2 * core + dest != me)
+        def _():
+            drained(out_stage.at[:, pl.ds(0, seq)], osend_sem.at[dest])
 
     @pl.when(has_prev)
     def _():
         mask_side(0).wait_send()
+        drained(h_ext.at[:, :, pl.ds(0, EDGE)], send_sem.at[0])
 
     @pl.when(has_next)
     def _():
         mask_side(1).wait_send()
-
-    @pl.loop(0, n_layers)
-    def _(layer):
-        @pl.loop(0, n_groups)
-        def _(grp):
-            @pl.when(has_prev)
-            def _():
-                halo_copy(layer, grp, 0).wait_send()
-
-            @pl.when(has_next)
-            def _():
-                halo_copy(layer, grp, 1).wait_send()
-
-    for half in range(2):
-        @pl.loop(0, n_groups)
-        def _(grp):
-            arrived(out_hbm.at[pl.ds(half * half_smp + grp * GROUP, GROUP)], orecv_sem.at[half, grp])
+        drained(h_ext.at[:, :, pl.ds(0, EDGE)], send_sem.at[1])
+
+    for dest in range(2):
+        arrived(out_hbm.at[pl.ds(dest * half_smp, half_smp)], orecv_sem.at[dest])
 
 
 def solution(mesh):
@@ -607,6 +626,8 @@
                 pltpu.VMEM(w_out.shape, bf16),
                 pltpu.VMEM(w_up.shape, bf16),
                 pltpu.VMEM(w_down.shape, bf16),
+                pltpu.VMEM(cond.shape, bf16),
+                pltpu.VMEM(atom_act.shape, bf16),
                 pltpu.VMEM((half_smp, own, width), bf16),
                 pltpu.VMEM((own, width), bf16),
                 pltpu.VMEM((8, 128), jnp.int32),
@@ -624,27 +645,26 @@
                 pltpu.VMEM((n_layers, width, width), bf16),
                 pltpu.VMEM((n_layers, 4 * width, width), bf16),
                 pltpu.VMEM((n_layers, width, 2 * width), bf16),
-                pltpu.VMEM((n_layers, width, width), f32),
                 pltpu.VMEM((GROUP, ext, width), bf16),
-                pltpu.VMEM((GROUP, width, n_blocks * 128), bf16),
-                pltpu.VMEM((GROUP, ext, width), bf16),
+                pltpu.VMEM((GROUP, n_blocks * 128, width), bf16),
                 pltpu.VMEM((GROUP, width, ext), bf16),
                 pltpu.VMEM((width, cols), f32),
                 pltpu.VMEM((2, 2, KEY_WINDOW, 128), f32),
                 pltpu.VMEM((2 * width, cols), bf16),
-                dma((6,)),
-                dma((n_layers, n_groups, 2)),
+                pltpu.VMEM((width, cols), bf16),
+                dma((12,)),
+                dma((2,)),
                 dma((n_layers, n_groups, 2)),
                 dma((2,)),
                 dma((2,)),
                 dma((4,)),
                 dma((4,)),
+                dma((2,)),
                 dma((2, n_groups)),
-                dma((2, n_groups)),
+                dma((2,)),
                 dma((2, n_layers)),
-                dma((2, n_layers)),
-                dma((2, n_groups)),
-                dma((2, n_groups)),
+                dma((2,)),
+                dma((2,)),
             ],
             compiler_params=pltpu.CompilerParams(
                 collective_id=0, has_side_effects=True, vmem_limit_bytes=60 * 1024 * 1024),

time: 40 us -> 37.5 us (0.938)
  Pallas kernels: 37.8 us -> 35.4 us
    pallas_call x1, Pallas kernels: 37.8 us -> 35.4 us  [device_fn(): pl.pallas_call(functools.partial(body, n_dev), out_shape=jax.ShapeDtypeSt...]
where the time goes in v4:
time: 37.5 us; the launch traced here: 37.3 us
  Pallas kernels  35.4 us (94%)
  local copies, waits for them, and re-layouts  1.87 us (5%)
    pallas_call x1, Pallas kernels, device_fn(): pl.pallas_call(functools.partial(body, n_dev), out_shape=jax.ShapeDtypeSt...  35.4 us
    unnamed x1, local copies, waits for them, and re-layouts  1.87 us

profile of v4, /device:TPU:0, one launch (start us, length us, event | category | flops | bytes accessed | tf_op | source)
XLA Modules:
  0.0 37.3 jit_solution(7549568839560062828)
XLA Ops:
  0.0 35.4 %shard_map.118 = bf16[32,64,128]{2,1,0:T(8,128)(2,1)} custom-call(bf16[32,64,128]{2,1,0:T(8,128)(2,1)} %act_hbm.1, bf16[64,128]{1,0:T(8,128)(2,1)} %cond_hbm.1, bf16[1024,128]{1,0:T(8,128)(2,1)} %bitcast.4, s32[1,64]{1,0:T(1,128)} %bitcast.5, bf16[3,128,768]{2,1,0:T(8,128)(2,1)} %wcond_hbm.1, f32[3,512]{1,0:T(4,128)} %bcond_ref.1, ...), custom_call_target="tpu_custom_call" | custom-call | tf_op jit(solution)/shard_map/pallas_call | solution.py:617
  35.4 1.9 %copy.14 = bf16[32,64,128]{2,1,0:T(8,128)(2,1)} copy(bf16[32,64,128]{2,1,0:T(8,128)(2,1)} %shard_map.118) | data formatting | bytes 1048576

commit v5 on v4

--- a/solution.py
+++ b/solution.py
@@ -40,7 +40,7 @@
          wout_hbm, wup_hbm, wdown_hbm, out_hbm,
          pair, wcond, wqkvg, wout, wup, wdown, cond_own, act,
          act_in, cond_in, mask_own, mask_in, bias_own, bias_in, out_stage,
-         res, h_cm, h_ext, tab, bias, wv_t, wg_t, wo_t, wu_t, wd_t,
+         res, h_cm, h_ext, tab, bias, wv_t, wg_t, wo_t, wu_t, wd_t, wc_t, bc_t,
          k_scr, q_scr, v_scr, o_scr, s_scr, m_scr, h_mid,
          in_sem, send_sem, recv_sem, csend_sem, crecv_sem, msend_sem, mrecv_sem, asend_sem, arecv_sem,
          bsend_sem, brecv_sem, osend_sem, orecv_sem):
@@ -167,6 +167,12 @@
     half = jnp.array(0.5, bf16)
 
     def weights(layer):
+        for idx, bias_idx in enumerate((0, None, 1, 2, None, 3)):
+            piece = wcond[layer, :, idx * width:(idx + 1) * width].T
+            wc_t[layer, idx * width:(idx + 1) * width, :] = piece if bias_idx is None else piece * half
+            if bias_idx is not None:
+                cell = bcond_ref[pl.ds(layer, 1), :][:, bias_idx * width:(bias_idx + 1) * width] * 0.5
+                bc_t[layer, bias_idx] = jnp.broadcast_to(cell, (own, width)).T
         wv_t[layer] = wqkvg[layer, :, 2 * width:3 * width].T
         wg_t[layer] = wqkvg[layer, :, 3 * width:].T * half
         wo_t[layer] = wout[layer].T
@@ -176,12 +182,10 @@
         for idx in range(2):
             wd_t[layer, :, idx * width:(idx + 1) * width] = wdown[layer, idx * width:(idx + 1) * width, :].T
 
-    for load in loads[2:]:
+    for load in loads[1:]:
         load.wait()
 
-    @pl.loop(0, n_layers)
-    def _(layer):
-        weights(layer)
+    weights(0)
 
     n_beyond = jnp.where(has_beyond, 1, 0)
     pl.semaphore_wait(barrier, 3 + n_beyond)
@@ -203,19 +207,38 @@
         for dest in range(2):
             push(*bias_push(dest, layer))
 
+    @pl.loop(1, n_layers)
+    def _(layer):
+        weights(layer)
+
     for slot in range(2):
         arrived(cond_in.at[pl.ds(slot * seq, seq)], crecv_sem.at[slot])
     cond_norm = norm(cond_in[...].astype(f32), -1).astype(bf16)
-    loads[1].wait()
 
     def tables(layer, first=0, last=6):
-        proj = mm(cond_norm, wcond[layer, :, first * width:last * width])
-        gates = bcond_ref[pl.ds(layer, 1), :]
+        proj = mm_nt(wc_t[layer, first * width:last * width], cond_norm)
+        yield
         for idx, bias_idx in list(enumerate((0, None, 1, 2, None, 3)))[first:last]:
-            piece = proj[:, (idx - first) * width:(idx - first + 1) * width]
+            piece = proj[(idx - first) * width:(idx - first + 1) * width]
             if bias_idx is not None:
-                piece = sigmoid(piece + gates[:, bias_idx * width:(bias_idx + 1) * width])
-            tab[layer, idx] = piece.T
+                piece = 0.5 * jnp.tanh(piece + bc_t[layer, bias_idx]) + 0.5
+            tab[layer, idx] = piece
+            yield
+
+    def idle(rounds):
+        for _ in range(rounds):
+            yield
+
+    def chain(*parts):
+        for part in parts:
+            yield from part
+
+    def interleave(*stages):
+        stages = list(stages)
+        while stages:
+            for stage in list(stages):
+                if next(stage, stages) is stages:
+                    stages.remove(stage)
 
     def both(vals):
         return jnp.concatenate([vals] * GROUP, axis=1)
@@ -265,12 +288,6 @@
         emit_h(0, grp, resid)
         yield
 
-    def enter_now(grp):
-        act_wait(grp)
-        for _ in enter(grp):
-            pass
-        halo_start(0, grp)
-
     def bias_wait(layer):
         for slot in range(2):
             arrived(bias_in.at[layer, slot], brecv_sem.at[slot, layer])
@@ -283,12 +300,13 @@
             bias[layer, blk] = ((nat + mask_bias[:, blk * QBLOCK:blk * QBLOCK + KEY_WINDOW]) * LOG2E).T
             yield
 
-    tables(0, 0, 2)
-    enter_now(0)
-    tables(0, 2, 6)
-    tables(1)
-    enter_now(1)
-    tables(2)
+    interleave(tables(0, 0, 2))
+    act_wait(0)
+    interleave(enter(0))
+    halo_start(0, 0)
+    act_wait(1)
+    interleave(enter(1), chain(tables(0, 2, 6), tables(1)))
+    halo_start(0, 1)
     for slot in range(1, 3):
         arrived(mask_in.at[slot], mrecv_sem.at[slot])
 
@@ -300,7 +318,9 @@
     def _():
         mask_side(1).start()
 
-    enter_now(2)
+    act_wait(2)
+    interleave(enter(2), tables(2))
+    halo_start(0, 2)
     @pl.when(has_prev)
     def _():
         arrived(mask_in.at[0], mrecv_sem.at[0])
@@ -313,9 +333,9 @@
                                 mask_in[3, 0:1, :EDGE], jnp.zeros((1, 256 - ext), jnp.int32)], axis=1)
     mask_bias = (mask_row.astype(f32) - 1.0) * 1e9
     bias_wait(0)
-    for _ in bias_table(0, mask_bias):
-        pass
-    enter_now(3)
+    act_wait(3)
+    interleave(enter(3), bias_table(0, mask_bias))
+    halo_start(0, 3)
 
     lane = lax.broadcasted_iota(jnp.int32, (1, width), 1)
     scale = head_dim ** -0.5 * LOG2E
@@ -503,21 +523,6 @@
         else:
             halo_start(layer + 1, grp)
 
-    def idle(rounds):
-        for _ in range(rounds):
-            yield
-
-    def chain(*parts):
-        for part in parts:
-            yield from part
-
-    def interleave(*stages):
-        stages = list(stages)
-        while stages:
-            for stage in list(stages):
-                if next(stage, stages) is stages:
-                    stages.remove(stage)
-
     def loop_body(idx, last, *extra):
         halo_wait(*split(idx + 1))
         interleave(chain(idle(1), finish(idx - 2, last)), chain(idle(0), mix(idx - 1)), attend(idx), chain(idle(2), project(idx + 1)), chain(idle(10), score_early()), *extra)
@@ -541,16 +546,21 @@
     loop_body(2, False, enter(7))
     halo_start(0, 7)
 
-    @pl.loop(3, 6)
+    @pl.loop(3, 7)
     def _(idx):
         loop_body(idx, False)
 
-    @pl.loop(6, 8)
+    bias_wait(1)
+    loop_body(7, False, bias_table(1, mask_bias))
+
+    @pl.loop(8, 12)
     def _(idx):
-        bias_wait(idx - 5)
-        loop_body(idx, False, bias_table(idx - 5, mask_bias))
-
-    @pl.loop(8, split_at + 2)
+        loop_body(idx, False)
+
+    bias_wait(2)
+    loop_body(12, False, bias_table(2, mask_bias))
+
+    @pl.loop(13, split_at + 2)
     def _(idx):
         loop_body(idx, False)
 
@@ -645,6 +655,8 @@
                 pltpu.VMEM((n_layers, width, width), bf16),
                 pltpu.VMEM((n_layers, 4 * width, width), bf16),
                 pltpu.VMEM((n_layers, width, 2 * width), bf16),
+                pltpu.VMEM((n_layers, 6 * width, width), bf16),
+                pltpu.VMEM((n_layers, 4, width, own), f32),
                 pltpu.VMEM((GROUP, ext, width), bf16),
                 pltpu.VMEM((GROUP, n_blocks * 128, width), bf16),
                 pltpu.VMEM((GROUP, width, ext), bf16),

time: 37.5 us -> 37.1 us (0.989)
  Pallas kernels: 35.4 us -> 35 us
where the time goes in v5:
time: 37.1 us; the launch traced here: 36.9 us
  Pallas kernels  35 us (94%)
  local copies, waits for them, and re-layouts  1.87 us (5%)
    pallas_call x1, Pallas kernels, device_fn(): pl.pallas_call(functools.partial(body, n_dev), out_shape=jax.ShapeDtypeSt...  35 us
    unnamed x1, local copies, waits for them, and re-layouts  1.87 us

profile of v5, /device:TPU:0, one launch (start us, length us, event | category | flops | bytes accessed | tf_op | source)
XLA Modules:
  0.0 36.9 jit_solution(11774285221138313562)
XLA Ops:
  0.0 35.0 %shard_map.118 = bf16[32,64,128]{2,1,0:T(8,128)(2,1)} custom-call(bf16[32,64,128]{2,1,0:T(8,128)(2,1)} %act_hbm.1, bf16[64,128]{1,0:T(8,128)(2,1)} %cond_hbm.1, bf16[1024,128]{1,0:T(8,128)(2,1)} %bitcast.4, s32[1,64]{1,0:T(1,128)} %bitcast.5, bf16[3,128,768]{2,1,0:T(8,128)(2,1)} %wcond_hbm.1, f32[3,512]{1,0:T(4,128)} %bcond_ref.1, ...), custom_call_target="tpu_custom_call" | custom-call | tf_op jit(solution)/shard_map/pallas_call | solution.py:627
  35.0 1.9 %copy.14 = bf16[32,64,128]{2,1,0:T(8,128)(2,1)} copy(bf16[32,64,128]{2,1,0:T(8,128)(2,1)} %shard_map.118) | data formatting | bytes 1048576

commit v6 on v5

--- a/solution.py
+++ b/solution.py
@@ -85,41 +85,47 @@
     def arrived(dst, rsem):
         pltpu.make_async_copy(dst, dst, rsem).wait()
 
+    barrier = pltpu.get_barrier_semaphore()
+
+    for other in range(4):
+        peer = 4 * plane + other
+
+        @pl.when(peer != me)
+        def _():
+            pl.semaphore_signal(barrier, inc=1, device_id={'sp': peer}, device_id_type=MESH)
+
+    beyond = chunk + 2 * core - 1
+    has_beyond = jnp.logical_and(beyond >= 0, beyond < 2 * n_planes)
+
+    @pl.when(has_beyond)
+    def _():
+        pl.semaphore_signal(barrier, inc=1, device_id={'sp': owner(beyond, row)}, device_id_type=MESH)
+
     loads = [pltpu.make_async_copy(src, dst, in_sem.at[pos]) for pos, (src, dst) in enumerate(
         [(pair_hbm, pair), (wcond_hbm, wcond), (wqkvg_hbm, wqkvg), (wout_hbm, wout), (wup_hbm, wup), (wdown_hbm, wdown),
          (cond_hbm, cond_own), (act_hbm, act)])]
     for load in loads:
         load.start()
 
-    zero_rows = jnp.zeros((GROUP, EDGE, width), bf16)
-
-    @pl.loop(0, n_layers)
-    def _(layer):
-        @pl.loop(0, n_groups)
-        def _(grp):
-            h_ext[layer, pl.ds(grp * GROUP, GROUP), 0:EDGE, :] = zero_rows
-            h_ext[layer, pl.ds(grp * GROUP, GROUP), EDGE + own:ext, :] = zero_rows
+    def clear(first, slot):
+        @pl.loop(0, n_layers)
+        def _(layer):
+            @pl.loop(0, n_groups)
+            def _(grp):
+                h_ext[layer, pl.ds(grp * GROUP, GROUP), first:first + EDGE, :] = jnp.zeros((GROUP, EDGE, width), bf16)
+
+        mask_in[slot] = jnp.zeros_like(mask_own)
+
+    @pl.when(jnp.logical_not(has_prev))
+    def _():
+        clear(0, 0)
+
+    @pl.when(jnp.logical_not(has_next))
+    def _():
+        clear(EDGE + own, 3)
 
     mask_own[...] = jnp.zeros_like(mask_own)
     mask_own[0:1, 0:seq] = mask_ref[...]
-    mask_in[0] = jnp.zeros_like(mask_own)
-    mask_in[3] = jnp.zeros_like(mask_own)
-
-    barrier = pltpu.get_barrier_semaphore()
-
-    for other in range(4):
-        peer = 4 * plane + other
-
-        @pl.when(peer != me)
-        def _():
-            pl.semaphore_signal(barrier, inc=1, device_id={'sp': peer}, device_id_type=MESH)
-
-    beyond = chunk + 2 * core - 1
-    has_beyond = jnp.logical_and(beyond >= 0, beyond < 2 * n_planes)
-
-    @pl.when(has_beyond)
-    def _():
-        pl.semaphore_signal(barrier, inc=1, device_id={'sp': owner(beyond, row)}, device_id_type=MESH)
 
     home = 2 * plane + row
 

time: 37.1 us -> 36.9 us (level)
  no operation moved by 1% of the time
where the time goes in v6:
time: 36.9 us; the launch traced here: 36.7 us
  Pallas kernels  34.8 us (94%)
  local copies, waits for them, and re-layouts  1.87 us (5%)
    pallas_call x1, Pallas kernels, device_fn(): pl.pallas_call(functools.partial(body, n_dev), out_shape=jax.ShapeDtypeSt...  34.8 us
    unnamed x1, local copies, waits for them, and re-layouts  1.87 us

profile of v6, /device:TPU:0, one launch (start us, length us, event | category | flops | bytes accessed | tf_op | source)
XLA Modules:
  0.0 36.7 jit_solution(5148443949544280558)
XLA Ops:
  0.0 34.8 %shard_map.118 = bf16[32,64,128]{2,1,0:T(8,128)(2,1)} custom-call(bf16[32,64,128]{2,1,0:T(8,128)(2,1)} %act_hbm.1, bf16[64,128]{1,0:T(8,128)(2,1)} %cond_hbm.1, bf16[1024,128]{1,0:T(8,128)(2,1)} %bitcast.4, s32[1,64]{1,0:T(1,128)} %bitcast.5, bf16[3,128,768]{2,1,0:T(8,128)(2,1)} %wcond_hbm.1, f32[3,512]{1,0:T(4,128)} %bcond_ref.1, ...), custom_call_target="tpu_custom_call" | custom-call | tf_op jit(solution)/shard_map/pallas_call | solution.py:633
  34.8 1.9 %copy.14 = bf16[32,64,128]{2,1,0:T(8,128)(2,1)} copy(bf16[32,64,128]{2,1,0:T(8,128)(2,1)} %shard_map.118) | data formatting | bytes 1048576

commit v7 on v6

--- a/solution.py
+++ b/solution.py
@@ -196,21 +196,21 @@
     n_beyond = jnp.where(has_beyond, 1, 0)
     pl.semaphore_wait(barrier, 3 + n_beyond)
 
-    for dest in range(2):
+    for dest in (1 - row, row):
         push(*cond_push(dest))
     for grp in range(3):
-        for dest in range(2):
+        for dest in (1 - row, row):
             push(*act_push(dest, grp))
         if grp == 0:
-            for dest in range(2):
+            for dest in (1 - row, row):
                 push(*mask_push(dest))
-    for dest in range(2):
+    for dest in (1 - row, row):
         push(*bias_push(dest, 0))
     for grp in range(3, n_groups):
-        for dest in range(2):
+        for dest in (1 - row, row):
             push(*act_push(dest, grp))
     for layer in range(1, n_layers):
-        for dest in range(2):
+        for dest in (1 - row, row):
             push(*bias_push(dest, layer))
 
     @pl.loop(1, n_layers)

time: 36.9 us -> 36.9 us (level)
  no operation moved by 1% of the time
where the time goes in v7:
time: 36.9 us; the launch traced here: 36.6 us
  Pallas kernels  34.8 us (94%)
  local copies, waits for them, and re-layouts  1.87 us (5%)
    pallas_call x1, Pallas kernels, device_fn(): pl.pallas_call(functools.partial(body, n_dev), out_shape=jax.ShapeDtypeSt...  34.8 us
    unnamed x1, local copies, waits for them, and re-layouts  1.87 us

profile of v7, /device:TPU:0, one launch (start us, length us, event | category | flops | bytes accessed | tf_op | source)
XLA Modules:
  0.0 36.6 jit_solution(16229350105614270939)
XLA Ops:
  0.0 34.8 %shard_map.118 = bf16[32,64,128]{2,1,0:T(8,128)(2,1)} custom-call(bf16[32,64,128]{2,1,0:T(8,128)(2,1)} %act_hbm.1, bf16[64,128]{1,0:T(8,128)(2,1)} %cond_hbm.1, bf16[1024,128]{1,0:T(8,128)(2,1)} %bitcast.4, s32[1,64]{1,0:T(1,128)} %bitcast.5, bf16[3,128,768]{2,1,0:T(8,128)(2,1)} %wcond_hbm.1, f32[3,512]{1,0:T(4,128)} %bcond_ref.1, ...), custom_call_target="tpu_custom_call" | custom-call | tf_op jit(solution)/shard_map/pallas_call | solution.py:633
  34.8 1.9 %copy.14 = bf16[32,64,128]{2,1,0:T(8,128)(2,1)} copy(bf16[32,64,128]{2,1,0:T(8,128)(2,1)} %shard_map.118) | data formatting | bytes 1048576

commit v8 on v7

--- a/solution.py
+++ b/solution.py
@@ -465,7 +465,7 @@
         layer, grp = split(idx)
         gate = mm(wg_t[layer], h_cm[grp])
         yield
-        yield from idle(2)
+        yield from idle(3)
         heads = []
         for head in range(n_heads):
             rows = slice(head * head_dim, (head + 1) * head_dim)

time: 36.9 us -> 36.7 us (level)
  no operation moved by 1% of the time
where the time goes in v8:
time: 36.7 us; the launch traced here: 36.5 us
  Pallas kernels  34.6 us (94%)
  local copies, waits for them, and re-layouts  1.87 us (5%)
    pallas_call x1, Pallas kernels, device_fn(): pl.pallas_call(functools.partial(body, n_dev), out_shape=jax.ShapeDtypeSt...  34.6 us
    unnamed x1, local copies, waits for them, and re-layouts  1.87 us

profile of v8, /device:TPU:0, one launch (start us, length us, event | category | flops | bytes accessed | tf_op | source)
XLA Modules:
  0.0 36.5 jit_solution(18292814815246166859)
XLA Ops:
  0.0 34.6 %shard_map.118 = bf16[32,64,128]{2,1,0:T(8,128)(2,1)} custom-call(bf16[32,64,128]{2,1,0:T(8,128)(2,1)} %act_hbm.1, bf16[64,128]{1,0:T(8,128)(2,1)} %cond_hbm.1, bf16[1024,128]{1,0:T(8,128)(2,1)} %bitcast.4, s32[1,64]{1,0:T(1,128)} %bitcast.5, bf16[3,128,768]{2,1,0:T(8,128)(2,1)} %wcond_hbm.1, f32[3,512]{1,0:T(4,128)} %bcond_ref.1, ...), custom_call_target="tpu_custom_call" | custom-call | tf_op jit(solution)/shard_map/pallas_call | solution.py:633
  34.6 1.9 %copy.14 = bf16[32,64,128]{2,1,0:T(8,128)(2,1)} copy(bf16[32,64,128]{2,1,0:T(8,128)(2,1)} %shard_map.118) | data formatting | bytes 1048576
